TPU v7x, 32 devices: a whole 2x2x4 slice. The times are simulated.
32 devices in a mesh: ta: 4 (over y, x), gz: 2 (over core), gy: 4 (over z).
Axes of the slice: x: 2, y: 2, z: 4, core: 2. Of those that a mesh axis runs over, the one named last changes fastest.
Arguments:
- source: float32 [2, 3, 8, 8, 512], P(None, None, 'ta', 'gz', 'gy'), may hold values from -40 to 40
- fat_links: bfloat16 [2, 4, 2, 3, 3, 8, 8, 512], P(None, None, None, None, None, 'ta', 'gz', 'gy'), may hold values from -1.25 to 1.25
- long_links: bfloat16 [2, 4, 2, 3, 3, 8, 8, 512], P(None, None, None, None, None, 'ta', 'gz', 'gy'), may hold values from -0.625 to 0.625
Outputs:
- solution: float32 [2, 3, 8, 8, 512], P(None, None, 'ta', 'gz', 'gy')
- true_residual: float32 [2, 3, 8, 8, 512], P(None, None, 'ta', 'gz', 'gy')
All inputs are finite; a program needn't handle non-finite values.
Results may differ from a plain program's by a relative error of at most 0.00085.
Values may be sent and summed in bfloat16 or wider, within the bound.
No kernel may reach another device: no remote copies, remote signals or barrier semaphores. Data moves between devices by JAX's collectives and lax.ppermute only.
A program may use at most 128 MiB of HBM per device.

v0:
```python
import jax
import jax.numpy as jnp
from jax import lax
from jax.sharding import PartitionSpec as P

NX = 32
ITERS = 8


mass_squared = 0.1


def passed_along(shard, axis, by):
    size = lax.axis_size(axis)
    return lax.ppermute(shard, axis, [(i, (i + by) % size) for i in range(size)])


def mat_vec(link, vector):
    real_a, imag_a = (link[0], link[1])
    real_v, imag_v = (vector[0], vector[1])
    real_o = jnp.sum(real_a * real_v[None] - imag_a * imag_v[None], axis=1)
    imag_o = jnp.sum(real_a * imag_v[None] + imag_a * real_v[None], axis=1)
    return jnp.stack([real_o, imag_o])


def adj_vec(link, vector):
    real_a, imag_a = (link[0], link[1])
    real_v, imag_v = (vector[0], vector[1])
    real_o = jnp.sum(real_a * real_v[:, None] + imag_a * imag_v[:, None], axis=0)
    imag_o = jnp.sum(real_a * imag_v[:, None] - imag_a * real_v[:, None], axis=0)
    return jnp.stack([real_o, imag_o])


def parity_mask(z_len, yx_len):
    zeds = jnp.arange(z_len, dtype=jnp.int32)[:, None]
    cells = jnp.arange(yx_len, dtype=jnp.int32)[None, :]
    return (zeds + cells // NX + cells % NX) % 2 == 1


def roll_x(field, shift):
    shape = field.shape
    folded = field.reshape(shape[:-1] + (shape[-1] // NX, NX))
    return jnp.roll(folded, shift, axis=-1).reshape(shape)


def time_terms(src, ahead, behind1, behind3, back1, back3, fat_dst, long_dst, select):
    rows = src.shape[2]
    extended = jnp.concatenate([src, ahead], axis=2)
    one = jnp.where(select, extended[:, :, 1 : rows + 1], extended[:, :, :rows])
    three = jnp.where(select, extended[:, :, 2 : rows + 2], extended[:, :, 1 : rows + 1])
    lower1 = jnp.concatenate([behind1, back1], axis=2)
    low1 = jnp.where(select, lower1[:, :, 1 : rows + 1], lower1[:, :, :rows])
    lower3 = jnp.concatenate([behind3, back3], axis=2)
    low3 = jnp.where(select, lower3[:, :, 1 : rows + 1], lower3[:, :, :rows])
    return mat_vec(fat_dst, one) + mat_vec(long_dst, three) - low1 - low3


def space_terms(src, ahead, behind1, behind3, back1, back3, fat_dst, long_dst, dim, unit):
    length = src.shape[dim]
    extended = jnp.concatenate([src, ahead], axis=dim)
    one = lax.slice_in_dim(extended, unit, unit + length, axis=dim)
    three = lax.slice_in_dim(extended, 3 * unit, 3 * unit + length, axis=dim)
    low1 = lax.slice_in_dim(jnp.concatenate([behind1, back1], axis=dim), 0, length, axis=dim)
    low3 = lax.slice_in_dim(jnp.concatenate([behind3, back3], axis=dim), 0, length, axis=dim)
    return mat_vec(fat_dst, one) + mat_vec(long_dst, three) - low1 - low3


def dslash(src, dst, srcp, fat_links, long_links, mask):
    select = mask if dst == 0 else jnp.logical_not(mask)
    rows, depth, width = (src.shape[2], src.shape[3], src.shape[4])
    backs = []
    for mu in range(4):
        backs.append(
            (
                adj_vec(fat_links[srcp, mu].astype(jnp.float32), src),
                adj_vec(long_links[srcp, mu].astype(jnp.float32), src),
            )
        )
    ahead_t = passed_along(src, "ta", -1)
    ahead_z = passed_along(src[:, :, :, :3], "gz", -1)
    ahead_y = passed_along(src[:, :, :, :, : 3 * NX], "gy", -1)
    sent_t = passed_along(
        jnp.concatenate([backs[0][0][:, :, rows - 1 :], backs[0][1]], axis=2), "ta", 1
    )
    sent_z = passed_along(
        jnp.concatenate(
            [backs[1][0][:, :, :, depth - 1 :], backs[1][1][:, :, :, depth - 3 :]], axis=3
        ),
        "gz",
        1,
    )
    sent_y = passed_along(
        jnp.concatenate(
            [backs[2][0][..., width - NX :], backs[2][1][..., width - 3 * NX :]], axis=4
        ),
        "gy",
        1,
    )
    rims_t = (sent_t[:, :, :1], sent_t[:, :, 1:])
    rims_z = (sent_z[:, :, :, :1], sent_z[:, :, :, 1:])
    rims_y = (sent_y[..., :NX], sent_y[..., NX:])
    total = time_terms(
        src,
        ahead_t,
        rims_t[0],
        rims_t[1],
        backs[0][0],
        backs[0][1],
        fat_links[dst, 0].astype(jnp.float32),
        long_links[dst, 0].astype(jnp.float32),
        select,
    )
    total = total + space_terms(
        src,
        ahead_z,
        rims_z[0],
        rims_z[1],
        backs[1][0],
        backs[1][1],
        fat_links[dst, 1].astype(jnp.float32),
        long_links[dst, 1].astype(jnp.float32),
        3,
        1,
    )
    total = total + space_terms(
        src,
        ahead_y,
        rims_y[0],
        rims_y[1],
        backs[2][0],
        backs[2][1],
        fat_links[dst, 2].astype(jnp.float32),
        long_links[dst, 2].astype(jnp.float32),
        4,
        NX,
    )
    fat_x = fat_links[dst, 3].astype(jnp.float32)
    long_x = long_links[dst, 3].astype(jnp.float32)
    total = total + (
        mat_vec(fat_x, roll_x(src, -1))
        + mat_vec(long_x, roll_x(src, -3))
        - roll_x(backs[3][0], 1)
        - roll_x(backs[3][1], 3)
    )
    return total


def two_products(residual, image):
    return lax.psum((jnp.sum(residual * residual), jnp.sum(residual * image)), ("ta", "gz", "gy"))


def per_device(source, fat_links, long_links):
    rows, depth, width = (source.shape[2], source.shape[3], source.shape[4])
    mask = parity_mask(depth, width)

    def normal_op(vector):
        odd_field = dslash(vector, 1, 0, fat_links, long_links, mask)
        return mass_squared * vector - dslash(odd_field, 0, 1, fat_links, long_links, mask)

    solution = jnp.zeros(source.shape, jnp.float32)
    residual = source
    image = normal_op(residual)
    norm_now, product = two_products(residual, image)
    alpha = norm_now / product
    direction, along = (residual, image)
    for step in range(ITERS):
        solution = solution + alpha * direction
        residual = residual - alpha * along
        if step + 1 < ITERS:
            image = normal_op(residual)
            norm_next, product = two_products(residual, image)
            ratio = norm_next / norm_now
            alpha = norm_next / (product - ratio * norm_next / alpha)
            direction = residual + ratio * direction
            along = image + ratio * along
            norm_now = norm_next
    return (solution, source - normal_op(solution))


def solution(mesh):
    in_specs = (
        P(None, None, "ta", "gz", "gy"),
        P(None, None, None, None, None, "ta", "gz", "gy"),
        P(None, None, None, None, None, "ta", "gz", "gy"),
    )
    out_specs = (P(None, None, "ta", "gz", "gy"), P(None, None, "ta", "gz", "gy"))
    return jax.shard_map(
        per_device, mesh=mesh, in_specs=in_specs, out_specs=out_specs, check_vma=False
    )
```

profile of v0, /device:TPU:0, one launch (start us, length us, event | category | flops | bytes accessed | tf_op | source)
XLA Modules:
  0.0 633.8 jit_solution(15613604482488652066)
XLA Ops:
  0.6 4.0 collective-permute-start
  4.6 3.6 collective-permute-start.4
  14.8 3.0 collective-permute-done.5
  20.2 3.0 collective-permute-start.10
  29.2 3.2 collective-permute-done.11
  34.5 40.8 %all-reduce.7 = (f32[]{:T(128)}, f32[]{:T(128)}) all-reduce(f32[]{:T(128)} %get-tuple-element.783, f32[]{:T(128)} %get-tuple-element.782), channel_id=1, replica_groups=mesh['ta'=4,'gz'=2,'gy'=4] {'ta','gz','gy'}, use_global_device_ids=true, to_apply=%region_1.2 | all-reduce | flops 2 | bytes 16 | tf_op jit(solution)/shard_map/psum | solution.py:149
  76.7 2.8 collective-permute-start.12
  86.5 3.6 collective-permute-done.17
  107.4 40.8 %all-reduce.6 = (f32[]{:T(128)}, f32[]{:T(128)}) all-reduce(f32[]{:T(128)} %get-tuple-element.757, f32[]{:T(128)} %get-tuple-element.756), channel_id=1, replica_groups=mesh['ta'=4,'gz'=2,'gy'=4] {'ta','gz','gy'}, use_global_device_ids=true, to_apply=%region_69.70 | all-reduce | flops 2 | bytes 16 | tf_op jit(solution)/shard_map/psum | solution.py:149
  152.7 2.9 collective-permute-start.24
  162.6 3.6 collective-permute-done.29
  183.3 40.3 %all-reduce.5 = (f32[]{:T(128)}, f32[]{:T(128)}) all-reduce(f32[]{:T(128)} %get-tuple-element.731, f32[]{:T(128)} %get-tuple-element.730), channel_id=1, replica_groups=mesh['ta'=4,'gz'=2,'gy'=4] {'ta','gz','gy'}, use_global_device_ids=true, to_apply=%region_137.138 | all-reduce | flops 2 | bytes 16 | tf_op jit(solution)/shard_map/psum | solution.py:149
  227.6 2.9 collective-permute-start.36
  237.5 3.6 collective-permute-done.41
  258.5 40.3 %all-reduce.4 = (f32[]{:T(128)}, f32[]{:T(128)}) all-reduce(f32[]{:T(128)} %get-tuple-element.705, f32[]{:T(128)} %get-tuple-element.704), channel_id=1, replica_groups=mesh['ta'=4,'gz'=2,'gy'=4] {'ta','gz','gy'}, use_global_device_ids=true, to_apply=%region_205.206 | all-reduce | flops 2 | bytes 16 | tf_op jit(solution)/shard_map/psum | solution.py:149
  302.7 2.9 collective-permute-start.48
  312.7 3.6 collective-permute-done.53
  333.4 40.3 %all-reduce.3 = (f32[]{:T(128)}, f32[]{:T(128)}) all-reduce(f32[]{:T(128)} %get-tuple-element.679, f32[]{:T(128)} %get-tuple-element.678), channel_id=1, replica_groups=mesh['ta'=4,'gz'=2,'gy'=4] {'ta','gz','gy'}, use_global_device_ids=true, to_apply=%region_273.274 | all-reduce | flops 2 | bytes 16 | tf_op jit(solution)/shard_map/psum | solution.py:149
  377.7 2.8 collective-permute-start.60
  387.6 3.6 collective-permute-done.65
  408.6 40.3 %all-reduce.2 = (f32[]{:T(128)}, f32[]{:T(128)}) all-reduce(f32[]{:T(128)} %get-tuple-element.653, f32[]{:T(128)} %get-tuple-element.652), channel_id=1, replica_groups=mesh['ta'=4,'gz'=2,'gy'=4] {'ta','gz','gy'}, use_global_device_ids=true, to_apply=%region_341.342 | all-reduce | flops 2 | bytes 16 | tf_op jit(solution)/shard_map/psum | solution.py:149
  452.9 3.0 collective-permute-start.72
  462.9 3.6 collective-permute-done.77
  469.5 2.4 collective-permute-start.82
  483.6 40.3 %all-reduce.1 = (f32[]{:T(128)}, f32[]{:T(128)}) all-reduce(f32[]{:T(128)} %get-tuple-element.627, f32[]{:T(128)} %get-tuple-element.626), channel_id=1, replica_groups=mesh['ta'=4,'gz'=2,'gy'=4] {'ta','gz','gy'}, use_global_device_ids=true, to_apply=%region_409.410 | all-reduce | flops 2 | bytes 16 | tf_op jit(solution)/shard_map/psum | solution.py:149
  528.6 2.8 collective-permute-start.84
  538.4 3.6 collective-permute-done.89
  545.1 2.5 collective-permute-start.94
  559.4 40.3 %all-reduce = (f32[]{:T(128)}, f32[]{:T(128)}) all-reduce(f32[]{:T(128)} %get-tuple-element.824, f32[]{:T(128)} %fusion.353), channel_id=1, replica_groups=mesh['ta'=4,'gz'=2,'gy'=4] {'ta','gz','gy'}, use_global_device_ids=true, to_apply=%region_477.478 | all-reduce | flops 2 | bytes 16 | tf_op jit(solution)/shard_map/psum | solution.py:149
  603.8 3.0 collective-permute-start.96
  613.9 3.6 collective-permute-done.101
  620.4 2.4 collective-permute-start.106
  (1165 shorter events, 199.6 us)
Async XLA Ops:
  0.6 13.1 %collective-permute-start = (f32[2,3,2,4,128]{4,3,2,1,0:T(4,128)}, f32[2,3,2,4,128]{4,3,2,1,0:T(4,128)S(1)}, u32[]{:S(2)}, u32[]{:S(2)}) collective-permute-start(f32[2,3,2,4,128]{4,3,2,1,0:T(4,128)} %param.3), channel_id=1, source_target_pairs={{0,24},{8,0},{16,8},{24,16},{1,25},{9,1},{17,9},{25,17},{2,26},{10... | collective-permute-start | bytes 73736 | tf_op jit(solution)/shard_map/ppermute | solution.py:15
  4.6 6.5 %collective-permute-start.2 = (f32[2,3,2,3,128]{4,3,2,1,0:T(4,128)}, f32[2,3,2,3,128]{4,3,2,1,0:T(4,128)S(1)}, u32[]{:S(2)}, u32[]{:S(2)}) collective-permute-start(f32[2,3,2,3,128]{4,3,2,1,0:T(4,128)} %bitcast.3617), channel_id=1, source_target_pairs={{0,4},{4,0},{1,5},{5,1},{2,6},{6,2},{3,7},{7,3},{8,12},{12,8},{9,1... | collective-permute-start | bytes 55304 | tf_op jit(solution)/shard_map/ppermute | solution.py:15
  4.6 9.2 %collective-permute-start.4 = (f32[2,3,2,4,96]{4,3,2,1,0:T(4,128)}, f32[2,3,2,4,96]{4,3,2,1,0:T(4,128)S(1)}, u32[]{:S(2)}, u32[]{:S(2)}) collective-permute-start(f32[2,3,2,4,96]{4,3,2,1,0:T(4,128)} %bitcast.3618), channel_id=1, source_target_pairs={{0,3},{1,0},{2,1},{3,2},{4,7},{5,4},{6,5},{7,6},{8,11},{9,8},{10,9... | collective-permute-start | bytes 55304 | tf_op jit(solution)/shard_map/ppermute | solution.py:15
  19.7 8.8 %collective-permute-start.6 = (f32[2,3,2,4,128]{4,3,2,1,0:T(4,128)S(1)}, f32[2,3,2,4,128]{4,3,2,1,0:T(4,128)S(1)}, u32[]{:S(2)}, u32[]{:S(2)}) collective-permute-start(f32[2,3,2,4,128]{4,3,2,1,0:T(4,128)S(1)} %fusion.154), channel_id=1, source_target_pairs={{0,24},{8,0},{16,8},{24,16},{1,25},{9,1},{17,9},{25,17},{2,26},{10... | collective-permute-start | bytes 73736 | tf_op jit(solution)/shard_map/ppermute | solution.py:15
  26.4 6.0 collective-permute-start.11
  76.7 9.1 %collective-permute-start.12 = (f32[2,3,2,4,128]{4,3,2,1,0:T(4,128)S(1)}, f32[2,3,2,4,128]{4,3,2,1,0:T(4,128)S(1)}, u32[]{:S(2)}, u32[]{:S(2)}) collective-permute-start(f32[2,3,2,4,128]{4,3,2,1,0:T(4,128)S(1)} %bitcast.3574), channel_id=1, source_target_pairs={{0,24},{8,0},{16,8},{24,16},{1,25},{9,1},{17,9},{25,17},{2,26},{10... | collective-permute-start | bytes 73736 | tf_op jit(solution)/shard_map/ppermute | solution.py:15
  84.1 5.9 collective-permute-start.17
  91.9 10.3 %collective-permute-start.18 = (f32[2,3,2,4,128]{4,3,2,1,0:T(4,128)S(1)}, f32[2,3,2,4,128]{4,3,2,1,0:T(4,128)S(1)}, u32[]{:S(2)}, u32[]{:S(2)}) collective-permute-start(f32[2,3,2,4,128]{4,3,2,1,0:T(4,128)S(1)} %fusion.141), channel_id=1, source_target_pairs={{0,24},{8,0},{16,8},{24,16},{1,25},{9,1},{17,9},{25,17},{2,26},{10... | collective-permute-start | bytes 73736 | tf_op jit(solution)/shard_map/ppermute | solution.py:15
  152.7 9.1 %collective-permute-start.24 = (f32[2,3,2,4,128]{4,3,2,1,0:T(4,128)S(1)}, f32[2,3,2,4,128]{4,3,2,1,0:T(4,128)S(1)}, u32[]{:S(2)}, u32[]{:S(2)}) collective-permute-start(f32[2,3,2,4,128]{4,3,2,1,0:T(4,128)S(1)} %bitcast.3581), channel_id=1, source_target_pairs={{0,24},{8,0},{16,8},{24,16},{1,25},{9,1},{17,9},{25,17},{2,26},{10... | collective-permute-start | bytes 73736 | tf_op jit(solution)/shard_map/ppermute | solution.py:15
  160.2 5.9 collective-permute-start.29
  168.1 10.3 %collective-permute-start.30 = (f32[2,3,2,4,128]{4,3,2,1,0:T(4,128)S(1)}, f32[2,3,2,4,128]{4,3,2,1,0:T(4,128)S(1)}, u32[]{:S(2)}, u32[]{:S(2)}) collective-permute-start(f32[2,3,2,4,128]{4,3,2,1,0:T(4,128)S(1)} %fusion.128), channel_id=1, source_target_pairs={{0,24},{8,0},{16,8},{24,16},{1,25},{9,1},{17,9},{25,17},{2,26},{10... | collective-permute-start | bytes 73736 | tf_op jit(solution)/shard_map/ppermute | solution.py:15
  227.6 9.2 %collective-permute-start.36 = (f32[2,3,2,4,128]{4,3,2,1,0:T(4,128)S(1)}, f32[2,3,2,4,128]{4,3,2,1,0:T(4,128)S(1)}, u32[]{:S(2)}, u32[]{:S(2)}) collective-permute-start(f32[2,3,2,4,128]{4,3,2,1,0:T(4,128)S(1)} %bitcast.3588), channel_id=1, source_target_pairs={{0,24},{8,0},{16,8},{24,16},{1,25},{9,1},{17,9},{25,17},{2,26},{10... | collective-permute-start | bytes 73736 | tf_op jit(solution)/shard_map/ppermute | solution.py:15
  235.1 5.9 collective-permute-start.41
  243.0 10.4 %collective-permute-start.42 = (f32[2,3,2,4,128]{4,3,2,1,0:T(4,128)S(1)}, f32[2,3,2,4,128]{4,3,2,1,0:T(4,128)S(1)}, u32[]{:S(2)}, u32[]{:S(2)}) collective-permute-start(f32[2,3,2,4,128]{4,3,2,1,0:T(4,128)S(1)} %fusion.115), channel_id=1, source_target_pairs={{0,24},{8,0},{16,8},{24,16},{1,25},{9,1},{17,9},{25,17},{2,26},{10... | collective-permute-start | bytes 73736 | tf_op jit(solution)/shard_map/ppermute | solution.py:15
  249.6 6.0 collective-permute-start.47
  302.7 9.2 %collective-permute-start.48 = (f32[2,3,2,4,128]{4,3,2,1,0:T(4,128)S(1)}, f32[2,3,2,4,128]{4,3,2,1,0:T(4,128)S(1)}, u32[]{:S(2)}, u32[]{:S(2)}) collective-permute-start(f32[2,3,2,4,128]{4,3,2,1,0:T(4,128)S(1)} %bitcast.3595), channel_id=1, source_target_pairs={{0,24},{8,0},{16,8},{24,16},{1,25},{9,1},{17,9},{25,17},{2,26},{10... | collective-permute-start | bytes 73736 | tf_op jit(solution)/shard_map/ppermute | solution.py:15
  310.3 5.9 collective-permute-start.53
  318.1 10.3 %collective-permute-start.54 = (f32[2,3,2,4,128]{4,3,2,1,0:T(4,128)S(1)}, f32[2,3,2,4,128]{4,3,2,1,0:T(4,128)S(1)}, u32[]{:S(2)}, u32[]{:S(2)}) collective-permute-start(f32[2,3,2,4,128]{4,3,2,1,0:T(4,128)S(1)} %fusion.102), channel_id=1, source_target_pairs={{0,24},{8,0},{16,8},{24,16},{1,25},{9,1},{17,9},{25,17},{2,26},{10... | collective-permute-start | bytes 73736 | tf_op jit(solution)/shard_map/ppermute | solution.py:15
  377.7 9.1 %collective-permute-start.60 = (f32[2,3,2,4,128]{4,3,2,1,0:T(4,128)S(1)}, f32[2,3,2,4,128]{4,3,2,1,0:T(4,128)S(1)}, u32[]{:S(2)}, u32[]{:S(2)}) collective-permute-start(f32[2,3,2,4,128]{4,3,2,1,0:T(4,128)S(1)} %bitcast.3602), channel_id=1, source_target_pairs={{0,24},{8,0},{16,8},{24,16},{1,25},{9,1},{17,9},{25,17},{2,26},{10... | collective-permute-start | bytes 73736 | tf_op jit(solution)/shard_map/ppermute | solution.py:15
  385.2 5.9 collective-permute-start.65
  393.1 10.5 %collective-permute-start.66 = (f32[2,3,2,4,128]{4,3,2,1,0:T(4,128)S(1)}, f32[2,3,2,4,128]{4,3,2,1,0:T(4,128)S(1)}, u32[]{:S(2)}, u32[]{:S(2)}) collective-permute-start(f32[2,3,2,4,128]{4,3,2,1,0:T(4,128)S(1)} %fusion.89), channel_id=1, source_target_pairs={{0,24},{8,0},{16,8},{24,16},{1,25},{9,1},{17,9},{25,17},{2,26},{10... | collective-permute-start | bytes 73736 | tf_op jit(solution)/shard_map/ppermute | solution.py:15
  399.7 6.1 collective-permute-start.71
  452.9 9.3 %collective-permute-start.72 = (f32[2,3,2,4,128]{4,3,2,1,0:T(4,128)S(1)}, f32[2,3,2,4,128]{4,3,2,1,0:T(4,128)S(1)}, u32[]{:S(2)}, u32[]{:S(2)}) collective-permute-start(f32[2,3,2,4,128]{4,3,2,1,0:T(4,128)S(1)} %bitcast.3609), channel_id=1, source_target_pairs={{0,24},{8,0},{16,8},{24,16},{1,25},{9,1},{17,9},{25,17},{2,26},{10... | collective-permute-start | bytes 73736 | tf_op jit(solution)/shard_map/ppermute | solution.py:15
  460.6 5.9 collective-permute-start.77
  468.4 10.3 %collective-permute-start.78 = (f32[2,3,2,4,128]{4,3,2,1,0:T(4,128)S(1)}, f32[2,3,2,4,128]{4,3,2,1,0:T(4,128)S(1)}, u32[]{:S(2)}, u32[]{:S(2)}) collective-permute-start(f32[2,3,2,4,128]{4,3,2,1,0:T(4,128)S(1)} %fusion.76), channel_id=1, source_target_pairs={{0,24},{8,0},{16,8},{24,16},{1,25},{9,1},{17,9},{25,17},{2,26},{10... | collective-permute-start | bytes 73736 | tf_op jit(solution)/shard_map/ppermute | solution.py:15
  475.0 6.0 collective-permute-start.83
  528.6 9.1 %collective-permute-start.84 = (f32[2,3,2,4,128]{4,3,2,1,0:T(4,128)S(1)}, f32[2,3,2,4,128]{4,3,2,1,0:T(4,128)S(1)}, u32[]{:S(2)}, u32[]{:S(2)}) collective-permute-start(f32[2,3,2,4,128]{4,3,2,1,0:T(4,128)S(1)} %get-tuple-element.825), channel_id=1, source_target_pairs={{0,24},{8,0},{16,8},{24,16},{1,25},{9,1},{17,9},{25,17},{2,26},{10... | collective-permute-start | bytes 73736 | tf_op jit(solution)/shard_map/ppermute | solution.py:15
  543.9 10.5 %collective-permute-start.90 = (f32[2,3,2,4,128]{4,3,2,1,0:T(4,128)S(1)}, f32[2,3,2,4,128]{4,3,2,1,0:T(4,128)S(1)}, u32[]{:S(2)}, u32[]{:S(2)}) collective-permute-start(f32[2,3,2,4,128]{4,3,2,1,0:T(4,128)S(1)} %fusion.63), channel_id=1, source_target_pairs={{0,24},{8,0},{16,8},{24,16},{1,25},{9,1},{17,9},{25,17},{2,26},{10... | collective-permute-start | bytes 73736 | tf_op jit(solution)/shard_map/ppermute | solution.py:15
  603.8 9.3 %collective-permute-start.96 = (f32[2,3,2,4,128]{4,3,2,1,0:T(4,128)S(1)}, f32[2,3,2,4,128]{4,3,2,1,0:T(4,128)S(1)}, u32[]{:S(2)}, u32[]{:S(2)}) collective-permute-start(f32[2,3,2,4,128]{4,3,2,1,0:T(4,128)S(1)} %bitcast.3624), channel_id=1, source_target_pairs={{0,24},{8,0},{16,8},{24,16},{1,25},{9,1},{17,9},{25,17},{2,26},{10... | collective-permute-start | bytes 73736 | tf_op jit(solution)/shard_map/ppermute | solution.py:15
  611.5 5.9 collective-permute-start.101
  619.0 10.6 %collective-permute-start.102 = (f32[2,3,2,4,128]{4,3,2,1,0:T(4,128)S(1)}, f32[2,3,2,4,128]{4,3,2,1,0:T(4,128)S(1)}, u32[]{:S(2)}, u32[]{:S(2)}) collective-permute-start(f32[2,3,2,4,128]{4,3,2,1,0:T(4,128)S(1)} %fusion.49), channel_id=1, source_target_pairs={{0,24},{8,0},{16,8},{24,16},{1,25},{9,1},{17,9},{25,17},{2,26},{10... | collective-permute-start | bytes 73736 | tf_op jit(solution)/shard_map/ppermute | solution.py:15
  624.8 6.0 collective-permute-start.107
  (170 other events, 374.6 us)
where the time goes:
time: 644 us; the launch traced here: 634 us
  blocking collectives  323 us (50%)
  starting transfers between devices  112 us (17%)
  local copies, waits for them, and re-layouts  66.9 us (10%)
  waiting for transfers between devices  64.7 us (10%)
  between operations  35.2 us (5%)
  other arithmetic  31.4 us (5%)
    psum x8, blocking collectives, two_products(): lax.psum((jnp.sum(residual * residual), jnp.sum(residual * image)), ('ta'...  323 us
    ppermute x108, starting transfers between devices, passed_along(): lax.ppermute(shard, axis, [(i, (i + by) % size) for i in range(size)])  112 us
    ppermute x108, waiting for transfers between devices, passed_along(): lax.ppermute(shard, axis, [(i, (i + by) % size) for i in range(size)])  64.7 us
    unnamed x116, local copies, waits for them, and re-layouts  23.1 us
    slice x72, local copies, waits for them, and re-layouts, dslash(): rims_t = (sent_t[:, :, :1], sent_t[:, :, 1:])  13.2 us
  transfers between devices with their start and end apart: 108, of which 43 were waited for; matrix products, arithmetic and copies ran while one was open for 8% of the time, Pallas kernels for 0%

commit v1 on v0

v1 whole, which is shorter than its diff:
```python
import jax
import jax.numpy as jnp
from jax import lax
from jax.experimental import pallas as pl
from jax.experimental.pallas import tpu as pltpu
from jax.sharding import PartitionSpec as P

NX = 32
ITERS = 8
STEPS = 2

mass_squared = 0.1
SCALE = 1.0 / 16.0

VMEM = pl.BlockSpec(memory_space=pltpu.VMEM)
PARAMS = pltpu.CompilerParams(vmem_limit_bytes=4 * 2**20)
AXES = ("ta", "gz", "gy")


def on_core(body, outs, *args):
    return pl.pallas_call(
        body,
        out_shape=tuple(jax.ShapeDtypeStruct(shape, jnp.float32) for shape in outs),
        in_specs=[VMEM] * len(args),
        out_specs=tuple(VMEM for _ in outs),
        compiler_params=PARAMS,
    )(*args)


def passed_along(shard, axis, by):
    size = lax.axis_size(axis)
    return lax.ppermute(shard, axis, [(i, (i + by) % size) for i in range(size)])


def rolled(tile, shift, axis):
    shift = shift % tile.shape[axis]
    return pltpu.roll(tile, shift, axis) if shift else tile


class Shifts:
    def __init__(self, rows, depth, width):
        self.rows, self.depth, self.width = (rows, depth, width)
        self.shape = (rows * depth, width)
        sub = lax.broadcasted_iota(jnp.int32, self.shape, 0)
        self.lane = lax.broadcasted_iota(jnp.int32, self.shape, 1)
        self.row = sub // depth
        self.plane = sub % depth
        self.x = self.lane % NX
        self.odd = (self.plane + self.lane // NX + self.x) % 2 == 1

    def select(self, dst):
        return self.odd if dst == 0 else jnp.logical_not(self.odd)

    def t_rows(self, own, other, by):
        if by == 0:
            return own
        near = self.row >= by if by > 0 else self.row < self.rows + by
        return rolled(jnp.where(near, own, other), -by * self.depth, 0)

    def t(self, own, other, by, dst):
        sel = self.select(dst)
        half = {1: (1, 0), 3: (2, 1), -1: (0, -1), -3: (-1, -2)}[by]
        return jnp.where(sel, self.t_rows(own, other, half[0]), self.t_rows(own, other, half[1]))

    def z(self, own, other, by):
        near = self.plane < self.depth - by if by > 0 else self.plane >= -by
        wrap = self.depth - by if by > 0 else -self.depth - by
        return jnp.where(near, rolled(own, -by, 0), rolled(other, wrap, 0))

    def y(self, own, other, by):
        lanes = by * NX
        near = self.lane >= lanes if by > 0 else self.lane < self.width + lanes
        return rolled(jnp.where(near, own, other), -lanes, 1)

    def x_(self, own, by):
        near = self.x < NX - by if by > 0 else self.x >= -by
        wrap = NX - by if by > 0 else -NX - by
        return jnp.where(near, rolled(own, -by, 1), rolled(own, wrap, 1))

    def hop(self, own, other, mu, by, dst):
        if mu == 0:
            return self.t(own, other, by, dst)
        if mu == 1:
            return self.z(own, other, by)
        if mu == 2:
            return self.y(own, other, by)
        return self.x_(own, by)


HOPS = tuple((mu, by) for mu in range(4) for by in (1, 3, -1, -3))


def link_tables(fat, long, near, dims):
    rows, depth, width = dims
    tile = (rows * depth, width)

    def body(fat_ref, long_ref, t_ref, z_ref, y_ref, out0, out1):
        shifts = Shifts(rows, depth, width)
        lows = (t_ref, z_ref, y_ref)
        for dst, out in ((0, out0), (1, out1)):

            def entry(i, carry):
                flip = 3 * (i % 3) + i // 3
                for k, (mu, by) in enumerate(HOPS):
                    kind = 0 if abs(by) == 1 else 1
                    ref = (fat_ref, long_ref)[kind]
                    for part in range(2):
                        if by > 0:
                            value = ref[dst, mu, 9 * part + i].astype(jnp.float32)
                            out[18 * k + 9 * part + i] = value
                        else:
                            own = ref[1 - dst, mu, 9 * part + i].astype(jnp.float32)
                            other = own
                            if mu < 3:
                                other = lows[mu][kind, 1 - dst, 9 * part + i].astype(jnp.float32)
                            value = shifts.hop(own, other, mu, by, dst)
                            out[18 * k + 9 * part + flip] = value if part else -value
                return carry

            lax.fori_loop(0, 9, entry, 0)

    return on_core(body, [(18 * len(HOPS),) + tile] * 2, fat, long, *near)


def hopping_sum(shifts, field, near, table, dst):
    total = [None] * 6
    for k, (mu, by) in enumerate(HOPS):
        ref = near[2 * mu + (0 if by > 0 else 1)] if mu < 3 else None
        hopped = [
            shifts.hop(field[c], ref[c] if mu < 3 else None, mu, by, dst) for c in range(6)
        ]
        for a in range(3):
            re = im = None
            for b in range(3):
                lre = table[18 * k + 3 * a + b]
                lim = table[18 * k + 9 + 3 * a + b]
                vre, vim = (hopped[b], hopped[3 + b])
                one, two = (lre * vre - lim * vim, lre * vim + lim * vre)
                re = one if re is None else re + one
                im = two if im is None else im + two
            total[a] = re if total[a] is None else total[a] + re
            total[3 + a] = im if total[3 + a] is None else total[3 + a] + im
    return total


def neighbours(field):
    zp = passed_along(field, "gz", -1)
    zm = zp if lax.axis_size("gz") == 2 else passed_along(field, "gz", 1)
    return (
        passed_along(field, "ta", -1),
        passed_along(field, "ta", 1),
        zp,
        zm,
        passed_along(field, "gy", -1),
        passed_along(field, "gy", 1),
    )


def odd_from_even(field, table, dims):
    def body(field_ref, tp, tm, zp, zm, yp, ym, table_ref, out):
        shifts = Shifts(*dims)
        for c, value in enumerate(
            hopping_sum(shifts, field_ref, (tp, tm, zp, zm, yp, ym), table_ref, 1)
        ):
            out[c] = value

    return on_core(body, [field.shape], field, *neighbours(field), table)[0]


def even_from_odd(field, start, table, dims, scale, base=None):
    def body(field_ref, tp, tm, zp, zm, yp, ym, table_ref, start_ref, *rest):
        shifts = Shifts(*dims)
        out = rest[-1]
        for c, value in enumerate(
            hopping_sum(shifts, field_ref, (tp, tm, zp, zm, yp, ym), table_ref, 0)
        ):
            image = scale * (mass_squared * start_ref[c] - value)
            out[c] = image if base is None else rest[0][c] - image

    extra = () if base is None else (base,)
    return on_core(body, [field.shape], field, *neighbours(field), table, start, *extra)[0]


def pairs_of(first):
    live = range(3 if first else 0, 6)
    return tuple((i, j) for i in live for j in live if i <= j)


def gram_parts(basis, copies):
    shape = basis[0].shape
    first = len(basis) == 3
    pairs = pairs_of(first)
    skip = 3 if first else 0

    def body(*refs):
        out = refs[-1]
        lane = lax.broadcasted_iota(jnp.int32, (8, 128), 1)
        row = lax.broadcasted_iota(jnp.int32, (8, 128), 0)
        packed = jnp.zeros((8, 128), jnp.float32)
        for n, (i, j) in enumerate(pairs):
            left, right = (refs[i - skip], refs[j - skip])
            tile = left[0] * right[0]
            for c in range(1, shape[0]):
                tile = tile + left[c] * right[c]
            value = jnp.sum(jnp.sum(tile, axis=0, keepdims=True), axis=1, keepdims=True)
            here = jnp.logical_and(row == n % 8, lane == n // 8)
            packed = jnp.where(here, value, packed)
        for k in range(copies):
            out[k] = packed

    return on_core(body, [(copies, 8, 128)], *basis)[0]


def block_update(sums, state, basis, solution):
    shape = basis[0].shape
    tile = shape[1:]
    first = state is None
    live = range(3 if first else 0, 6)
    before = () if first else (state, solution)

    def body(sums_ref, *refs):
        refs = list(refs)
        vectors = {i: refs.pop(0) for i in live}
        if not first:
            state_ref, solution_ref = (refs.pop(0), refs.pop(0))
            norm_before, alpha_before = (state_ref[0], state_ref[1])
        state_out, x_out, r_out, p_out, q_out, w_out = refs
        total = sums_ref[0]
        for k in range(1, sums_ref.shape[0]):
            total = total + sums_ref[k]
        gram = {}
        for n, (i, j) in enumerate(pairs_of(first)):
            value = jnp.broadcast_to(total[n % 8 : n % 8 + 1, n // 8 : n // 8 + 1], tile)
            gram[i, j] = gram[j, i] = value

        def add(a, b):
            return b if a is None else a if b is None else a + b

        def times(s, vec):
            return {i: s * v for i, v in vec.items()}

        def plus(u, v):
            return {i: add(u.get(i), v.get(i)) for i in sorted(set(u) | set(v))}

        def dot(u, v):
            out = None
            for i, a in u.items():
                part = None
                for j, b in v.items():
                    part = add(part, gram[i, j] * b)
                out = add(out, a * part)
            return out

        def applied(u):
            out = {}
            for i, a in u.items():
                if i == 0:
                    out = plus(out, {1: a})
                elif i == 1:
                    share = a / alpha_before
                    out = plus(out, {2: share, 4: share * (-1.0 / SCALE)})
                elif i in (3, 4):
                    out = plus(out, {i + 1: a * (1.0 / SCALE)})
            return out

        residual = {3: jnp.ones(tile, jnp.float32)}
        norm = gram[3, 3]
        direction = residual if first else {0: norm / norm_before, **residual}
        gain = {}
        for step in range(STEPS):
            if step:
                norm_next = dot(residual, residual)
                direction = plus(residual, times(norm_next / norm, direction))
                norm = norm_next
            image = applied(direction)
            alpha = norm / dot(direction, image)
            gain = plus(gain, times(alpha, direction))
            last = residual
            residual = plus(residual, times(-alpha, image))
        state_out[0] = norm
        state_out[1] = alpha
        shown = ((r_out, residual), (p_out, direction), (q_out, image), (w_out, applied(last)))
        for c in range(shape[0]):
            values = {i: vectors[i][c] for i in live}
            grown = sum(s * values[i] for i, s in gain.items())
            x_out[c] = grown if first else solution_ref[c] + grown
            for out, coefs in shown:
                out[c] = sum(s * values[i] for i, s in coefs.items())

    outs = [(2,) + tile] + [shape] * 5
    return on_core(body, outs, sums, *basis, *before)


def per_device(source, fat_links, long_links):
    rows, depth, width = source.shape[2:]
    dims = (rows, depth, width)
    tile = (rows * depth, width)
    field = source.reshape((6,) + tile)
    fat = fat_links.reshape((2, 4, 18) + tile)
    long = long_links.reshape((2, 4, 18) + tile)
    near = [
        passed_along(jnp.stack([fat[:, mu], long[:, mu]]), axis, 1)
        for mu, axis in enumerate(AXES)
    ]
    even_table, odd_table = link_tables(fat, long, near, dims)

    devices = 1
    for axis in AXES:
        devices *= lax.axis_size(axis)

    def powers(vector):
        odd = odd_from_even(vector, odd_table, dims)
        return even_from_odd(odd, vector, even_table, dims, SCALE)

    solution = state = None
    residual = field
    back = ()
    for _ in range(ITERS // STEPS):
        one = powers(residual)
        two = powers(one)
        basis = back + (residual, one, two)
        parts = gram_parts(basis, devices)
        sums = lax.all_to_all(parts, AXES, 0, 0, tiled=True)
        state, solution, residual, *back = block_update(sums, state, basis, solution)
        back = tuple(back)
    odd = odd_from_even(solution, odd_table, dims)
    true = even_from_odd(odd, solution, even_table, dims, 1.0, base=field)
    return (solution.reshape(source.shape), true.reshape(source.shape))


def solution(mesh):
    in_specs = (
        P(None, None, "ta", "gz", "gy"),
        P(None, None, None, None, None, "ta", "gz", "gy"),
        P(None, None, None, None, None, "ta", "gz", "gy"),
    )
    out_specs = (P(None, None, "ta", "gz", "gy"), P(None, None, "ta", "gz", "gy"))
    return jax.shard_map(
        per_device, mesh=mesh, in_specs=in_specs, out_specs=out_specs, check_vma=False
    )
```

time: 644 us -> 217 us (0.34); the launches traced: 634 us -> 217 us
  blocking collectives: 323 us -> 44.6 us
  local copies, waits for them, and re-layouts: 66.9 us -> 2.96 us
  between operations: 35.2 us -> 0.95 us
  other arithmetic: 31.4 us -> 0.05 us
  starting transfers between devices: 112 us -> 83.9 us
  waiting for transfers between devices: 64.7 us -> 76.5 us
  Pallas kernels: 0 us -> 7.78 us
    psum x8 -> x0, blocking collectives: 323 us -> none  [two_products(): lax.psum((jnp.sum(residual * residual), jnp.sum(residual * image)), ('ta'...]
    all_to_all x0 -> x4, blocking collectives: none -> 44.6 us  [per_device(): sums = lax.all_to_all(parts, AXES, 0, 0, tiled=True)]
    ppermute x108 -> x93, starting transfers between devices: 112 us -> 83.9 us  [passed_along(): lax.ppermute(shard, axis, [(i, (i + by) % size) for i in range(size)])]
    slice x216 -> x0, local copies, waits for them, and re-layouts: 22.6 us -> none  [the longest x72 13.2 us: dslash(): rims_t = (sent_t[:, :, :1], sent_t[:, :, 1:])]
    unnamed x116 -> x8, local copies, waits for them, and re-layouts: 23.1 us -> 2.88 us
    reduce_sum x168 -> x0, other arithmetic: 16.2 us -> none  [the longest x8 6.04 us: two_products(): jnp.sum(residual * image)]
    ppermute x108 -> x93, waiting for transfers between devices: 64.7 us -> 76.5 us  [passed_along(): lax.ppermute(shard, axis, [(i, (i + by) % size) for i in range(size)])]
    concatenate x126 -> x0, other arithmetic: 10.8 us -> none  [the longest x72 8.79 us: roll_x(): return jnp.roll(folded, shift, axis=-1).reshape(shape)]
  transfers between devices with their start and end apart: 108 -> 93, of which waited for: 43 -> 43; matrix products, arithmetic and copies ran while one was open for 8% -> 0% of each run, Pallas kernels for 0% -> 1%
where the time goes in v1:
time: 217 us
  starting transfers between devices  83.9 us (39%)
  waiting for transfers between devices  76.5 us (35%)
  blocking collectives  44.6 us (21%)
  Pallas kernels  7.78 us (4%)
  local copies, waits for them, and re-layouts  2.96 us (1%)
    ppermute x93, starting transfers between devices, passed_along(): lax.ppermute(shard, axis, [(i, (i + by) % size) for i in range(size)])  83.9 us
    ppermute x93, waiting for transfers between devices, passed_along(): lax.ppermute(shard, axis, [(i, (i + by) % size) for i in range(size)])  76.5 us
    all_to_all x4, blocking collectives, per_device(): sums = lax.all_to_all(parts, AXES, 0, 0, tiled=True)  44.6 us
    pallas_call x27, Pallas kernels, on_core(): pl.pallas_call(body, out_shape=tuple((jax.ShapeDtypeStruct(shape, jnp.flo...  7.78 us
  transfers between devices with their start and end apart: 93, of which 43 were waited for; matrix products, arithmetic and copies ran while one was open for 0% of the time, Pallas kernels for 1%

profile of v1, /device:TPU:0, one launch (start us, length us, event | category | flops | bytes accessed | tf_op | source)
XLA Modules:
  0.0 216.8 jit_solution(10795399349843462872)
XLA Ops:
  3.4 2.6 %collective-permute-start.7 = (bf16[2,2,18,8,128]{4,3,2,1,0:T(8,128)(2,1)S(1)}, bf16[2,2,18,8,128]{4,3,2,1,0:T(8,128)(2,1)S(1)}, u32[]{:S(2)}, u32[]{:S(2)}) collective-permute-start(bf16[2,2,18,8,128]{4,3,2,1,0:T(8,128)(2,1)S(1)} %pad_maximum_fusion.2), channel_id=1, source_target_pairs={{0,1},{1,2},{2,3},{3,0},{4,5},{5,6},{6,7},{7,4},{8,9},{9,10},{10,1... | collective-permute-start | bytes 442376 | tf_op jit(solution)/shard_map/ppermute | solution.py:32
  9.7 2.9 %collective-permute-done.7.y_ref = bf16[2,2,18,8,128]{4,3,2,1,0:T(8,128)(2,1)S(1)} collective-permute-done((bf16[2,2,18,8,128]{4,3,2,1,0:T(8,128)(2,1)S(1)}, bf16[2,2,18,8,128]{4,3,2,1,0:T(8,128)(2,1)S(1)}, u32[]{:S(2)}, u32[]{:S(2)}) %collective-permute-start.7) | collective-permute-done | bytes 147488 | tf_op jit(solution)/shard_map/ppermute | solution.py:32
  16.7 3.2 %collective-permute-done.4.ym = f32[6,8,128]{2,1,0:T(8,128)S(1)} collective-permute-done((f32[6,8,128]{2,1,0:T(8,128)S(1)}, f32[6,8,128]{2,1,0:T(8,128)S(1)}, u32[]{:S(2)}, u32[]{:S(2)}) %collective-permute-start.4) | collective-permute-done | bytes 24608 | tf_op jit(solution)/shard_map/ppermute | solution.py:32
  20.3 2.0 collective-permute-start.12
  22.3 2.4 %collective-permute-start.8 = (f32[6,8,128]{2,1,0:T(8,128)S(1)}, f32[6,8,128]{2,1,0:T(8,128)S(1)}, u32[]{:S(2)}, u32[]{:S(2)}) collective-permute-start(f32[6,8,128]{2,1,0:T(8,128)S(1)} %shard_map.51.field_ref), channel_id=1, source_target_pairs={{0,24},{8,0},{16,8},{24,16},{1,25},{9,1},{17,9},{25,17},{2,26},{10... | collective-permute-start | bytes 73736 | tf_op jit(solution)/shard_map/ppermute | solution.py:32
  26.3 3.2 %collective-permute-done.9.tm = f32[6,8,128]{2,1,0:T(8,128)S(1)} collective-permute-done((f32[6,8,128]{2,1,0:T(8,128)S(1)}, f32[6,8,128]{2,1,0:T(8,128)S(1)}, u32[]{:S(2)}, u32[]{:S(2)}) %collective-permute-start.9) | collective-permute-done | bytes 24608 | tf_op jit(solution)/shard_map/ppermute | solution.py:32
  29.8 2.0 collective-permute-start.14
  35.6 3.7 %collective-permute-done.17.ym = f32[6,8,128]{2,1,0:T(8,128)S(1)} collective-permute-done((f32[6,8,128]{2,1,0:T(8,128)S(1)}, f32[6,8,128]{2,1,0:T(8,128)S(1)}, u32[]{:S(2)}, u32[]{:S(2)}) %collective-permute-start.17) | collective-permute-done | bytes 24608 | tf_op jit(solution)/shard_map/ppermute | solution.py:32
  47.6 10.4 %all_to_all.20.sums_ref = f32[32,8,128]{2,1,0:T(8,128)S(1)} all-to-all(f32[32,8,128]{2,1,0:T(8,128)S(1)} %shard_map.55), channel_id=1, replica_groups=mesh['ta'=4,'gz'=2,'gy'=4] {'ta','gz','gy'}, dimensions={0} | all-to-all | bytes 262144 | tf_op jit(solution)/shard_map/all_to_all | solution.py:323
  64.1 3.0 %collective-permute-done.27.ym = f32[6,8,128]{2,1,0:T(8,128)S(1)} collective-permute-done((f32[6,8,128]{2,1,0:T(8,128)S(1)}, f32[6,8,128]{2,1,0:T(8,128)S(1)}, u32[]{:S(2)}, u32[]{:S(2)}) %collective-permute-start.27) | collective-permute-done | bytes 24608 | tf_op jit(solution)/shard_map/ppermute | solution.py:32
  71.4 2.2 %collective-permute-done.29.tm = f32[6,8,128]{2,1,0:T(8,128)S(1)} collective-permute-done((f32[6,8,128]{2,1,0:T(8,128)S(1)}, f32[6,8,128]{2,1,0:T(8,128)S(1)}, u32[]{:S(2)}, u32[]{:S(2)}) %collective-permute-start.29) | collective-permute-done | bytes 24608 | tf_op jit(solution)/shard_map/ppermute | solution.py:32
  75.4 2.4 %collective-permute-start.33 = (f32[6,8,128]{2,1,0:T(8,128)S(1)}, f32[6,8,128]{2,1,0:T(8,128)S(1)}, u32[]{:S(2)}, u32[]{:S(2)}) collective-permute-start(f32[6,8,128]{2,1,0:T(8,128)S(1)} %shard_map.58.field_ref.start_ref.refs_4_), channel_id=1, source_target_pairs={{0,24},{8,0},{16,8},{24,16},{1,25},{9,1},{17,9},{25,17},{2,26},{10... | collective-permute-start | bytes 73736 | tf_op jit(solution)/shard_map/ppermute | solution.py:32
  80.1 2.5 %collective-permute-done.34.tm = f32[6,8,128]{2,1,0:T(8,128)S(1)} collective-permute-done((f32[6,8,128]{2,1,0:T(8,128)S(1)}, f32[6,8,128]{2,1,0:T(8,128)S(1)}, u32[]{:S(2)}, u32[]{:S(2)}) %collective-permute-start.34) | collective-permute-done | bytes 24608 | tf_op jit(solution)/shard_map/ppermute | solution.py:32
  84.0 2.7 %collective-permute-start.38 = (f32[6,8,128]{2,1,0:T(8,128)S(1)}, f32[6,8,128]{2,1,0:T(8,128)S(1)}, u32[]{:S(2)}, u32[]{:S(2)}) collective-permute-start(f32[6,8,128]{2,1,0:T(8,128)S(1)} %shard_map.59.field_ref), channel_id=1, source_target_pairs={{0,24},{8,0},{16,8},{24,16},{1,25},{9,1},{17,9},{25,17},{2,26},{10... | collective-permute-start | bytes 73736 | tf_op jit(solution)/shard_map/ppermute | solution.py:32
  89.0 2.4 %collective-permute-done.39.tm = f32[6,8,128]{2,1,0:T(8,128)S(1)} collective-permute-done((f32[6,8,128]{2,1,0:T(8,128)S(1)}, f32[6,8,128]{2,1,0:T(8,128)S(1)}, u32[]{:S(2)}, u32[]{:S(2)}) %collective-permute-start.39) | collective-permute-done | bytes 24608 | tf_op jit(solution)/shard_map/ppermute | solution.py:32
  93.0 11.4 %all_to_all.21.sums_ref = f32[32,8,128]{2,1,0:T(8,128)S(1)} all-to-all(f32[32,8,128]{2,1,0:T(8,128)S(1)} %shard_map.61), channel_id=1, replica_groups=mesh['ta'=4,'gz'=2,'gy'=4] {'ta','gz','gy'}, dimensions={0} | all-to-all | bytes 262144 | tf_op jit(solution)/shard_map/all_to_all | solution.py:323
  110.5 3.0 %collective-permute-done.47.ym = f32[6,8,128]{2,1,0:T(8,128)S(1)} collective-permute-done((f32[6,8,128]{2,1,0:T(8,128)S(1)}, f32[6,8,128]{2,1,0:T(8,128)S(1)}, u32[]{:S(2)}, u32[]{:S(2)}) %collective-permute-start.47) | collective-permute-done | bytes 24608 | tf_op jit(solution)/shard_map/ppermute | solution.py:32
  117.8 2.2 %collective-permute-done.49.tm = f32[6,8,128]{2,1,0:T(8,128)S(1)} collective-permute-done((f32[6,8,128]{2,1,0:T(8,128)S(1)}, f32[6,8,128]{2,1,0:T(8,128)S(1)}, u32[]{:S(2)}, u32[]{:S(2)}) %collective-permute-start.49) | collective-permute-done | bytes 24608 | tf_op jit(solution)/shard_map/ppermute | solution.py:32
  121.8 2.4 %collective-permute-start.53 = (f32[6,8,128]{2,1,0:T(8,128)S(1)}, f32[6,8,128]{2,1,0:T(8,128)S(1)}, u32[]{:S(2)}, u32[]{:S(2)}) collective-permute-start(f32[6,8,128]{2,1,0:T(8,128)S(1)} %shard_map.64.field_ref.start_ref.refs_4_), channel_id=1, source_target_pairs={{0,24},{8,0},{16,8},{24,16},{1,25},{9,1},{17,9},{25,17},{2,26},{10... | collective-permute-start | bytes 73736 | tf_op jit(solution)/shard_map/ppermute | solution.py:32
  126.5 2.5 %collective-permute-done.54.tm = f32[6,8,128]{2,1,0:T(8,128)S(1)} collective-permute-done((f32[6,8,128]{2,1,0:T(8,128)S(1)}, f32[6,8,128]{2,1,0:T(8,128)S(1)}, u32[]{:S(2)}, u32[]{:S(2)}) %collective-permute-start.54) | collective-permute-done | bytes 24608 | tf_op jit(solution)/shard_map/ppermute | solution.py:32
  130.4 2.7 %collective-permute-start.58 = (f32[6,8,128]{2,1,0:T(8,128)S(1)}, f32[6,8,128]{2,1,0:T(8,128)S(1)}, u32[]{:S(2)}, u32[]{:S(2)}) collective-permute-start(f32[6,8,128]{2,1,0:T(8,128)S(1)} %shard_map.65.field_ref), channel_id=1, source_target_pairs={{0,24},{8,0},{16,8},{24,16},{1,25},{9,1},{17,9},{25,17},{2,26},{10... | collective-permute-start | bytes 73736 | tf_op jit(solution)/shard_map/ppermute | solution.py:32
  135.4 2.4 %collective-permute-done.59.tm = f32[6,8,128]{2,1,0:T(8,128)S(1)} collective-permute-done((f32[6,8,128]{2,1,0:T(8,128)S(1)}, f32[6,8,128]{2,1,0:T(8,128)S(1)}, u32[]{:S(2)}, u32[]{:S(2)}) %collective-permute-start.59) | collective-permute-done | bytes 24608 | tf_op jit(solution)/shard_map/ppermute | solution.py:32
  139.4 11.4 %all_to_all.22.sums_ref = f32[32,8,128]{2,1,0:T(8,128)S(1)} all-to-all(f32[32,8,128]{2,1,0:T(8,128)S(1)} %shard_map.67), channel_id=1, replica_groups=mesh['ta'=4,'gz'=2,'gy'=4] {'ta','gz','gy'}, dimensions={0} | all-to-all | bytes 262144 | tf_op jit(solution)/shard_map/all_to_all | solution.py:323
  156.9 3.0 %collective-permute-done.67.ym = f32[6,8,128]{2,1,0:T(8,128)S(1)} collective-permute-done((f32[6,8,128]{2,1,0:T(8,128)S(1)}, f32[6,8,128]{2,1,0:T(8,128)S(1)}, u32[]{:S(2)}, u32[]{:S(2)}) %collective-permute-start.67) | collective-permute-done | bytes 24608 | tf_op jit(solution)/shard_map/ppermute | solution.py:32
  164.2 2.2 %collective-permute-done.69.tm = f32[6,8,128]{2,1,0:T(8,128)S(1)} collective-permute-done((f32[6,8,128]{2,1,0:T(8,128)S(1)}, f32[6,8,128]{2,1,0:T(8,128)S(1)}, u32[]{:S(2)}, u32[]{:S(2)}) %collective-permute-start.69) | collective-permute-done | bytes 24608 | tf_op jit(solution)/shard_map/ppermute | solution.py:32
  168.2 2.4 %collective-permute-start.73 = (f32[6,8,128]{2,1,0:T(8,128)S(1)}, f32[6,8,128]{2,1,0:T(8,128)S(1)}, u32[]{:S(2)}, u32[]{:S(2)}) collective-permute-start(f32[6,8,128]{2,1,0:T(8,128)S(1)} %shard_map.70.field_ref.start_ref.refs_4_), channel_id=1, source_target_pairs={{0,24},{8,0},{16,8},{24,16},{1,25},{9,1},{17,9},{25,17},{2,26},{10... | collective-permute-start | bytes 73736 | tf_op jit(solution)/shard_map/ppermute | solution.py:32
  172.9 2.5 %collective-permute-done.74.tm = f32[6,8,128]{2,1,0:T(8,128)S(1)} collective-permute-done((f32[6,8,128]{2,1,0:T(8,128)S(1)}, f32[6,8,128]{2,1,0:T(8,128)S(1)}, u32[]{:S(2)}, u32[]{:S(2)}) %collective-permute-start.74) | collective-permute-done | bytes 24608 | tf_op jit(solution)/shard_map/ppermute | solution.py:32
  176.8 2.7 %collective-permute-start.78 = (f32[6,8,128]{2,1,0:T(8,128)S(1)}, f32[6,8,128]{2,1,0:T(8,128)S(1)}, u32[]{:S(2)}, u32[]{:S(2)}) collective-permute-start(f32[6,8,128]{2,1,0:T(8,128)S(1)} %shard_map.71.field_ref), channel_id=1, source_target_pairs={{0,24},{8,0},{16,8},{24,16},{1,25},{9,1},{17,9},{25,17},{2,26},{10... | collective-permute-start | bytes 73736 | tf_op jit(solution)/shard_map/ppermute | solution.py:32
  181.8 2.4 %collective-permute-done.79.tm = f32[6,8,128]{2,1,0:T(8,128)S(1)} collective-permute-done((f32[6,8,128]{2,1,0:T(8,128)S(1)}, f32[6,8,128]{2,1,0:T(8,128)S(1)}, u32[]{:S(2)}, u32[]{:S(2)}) %collective-permute-start.79) | collective-permute-done | bytes 24608 | tf_op jit(solution)/shard_map/ppermute | solution.py:32
  185.8 11.4 %all_to_all.23.sums_ref = f32[32,8,128]{2,1,0:T(8,128)S(1)} all-to-all(f32[32,8,128]{2,1,0:T(8,128)S(1)} %shard_map.73), channel_id=1, replica_groups=mesh['ta'=4,'gz'=2,'gy'=4] {'ta','gz','gy'}, dimensions={0} | all-to-all | bytes 262144 | tf_op jit(solution)/shard_map/all_to_all | solution.py:323
  204.1 3.0 %collective-permute-done.87.ym = f32[6,8,128]{2,1,0:T(8,128)S(1)} collective-permute-done((f32[6,8,128]{2,1,0:T(8,128)}, f32[6,8,128]{2,1,0:T(8,128)S(1)}, u32[]{:S(2)}, u32[]{:S(2)}) %collective-permute-start.87) | collective-permute-done | bytes 24608 | tf_op jit(solution)/shard_map/ppermute | solution.py:32
  212.2 2.2 %collective-permute-done.89.tm = f32[6,8,128]{2,1,0:T(8,128)S(1)} collective-permute-done((f32[6,8,128]{2,1,0:T(8,128)S(1)}, f32[6,8,128]{2,1,0:T(8,128)S(1)}, u32[]{:S(2)}, u32[]{:S(2)}) %collective-permute-start.89) | collective-permute-done | bytes 24608 | tf_op jit(solution)/shard_map/ppermute | solution.py:32
  (199 shorter events, 98.1 us)
Async XLA Ops:
  2.8 6.8 %collective-permute-start.6 = (bf16[2,2,18,8,128]{4,3,2,1,0:T(8,128)(2,1)S(1)}, bf16[2,2,18,8,128]{4,3,2,1,0:T(8,128)(2,1)S(1)}, u32[]{:S(2)}, u32[]{:S(2)}) collective-permute-start(bf16[2,2,18,8,128]{4,3,2,1,0:T(8,128)(2,1)S(1)} %pad_maximum_fusion.1), channel_id=1, source_target_pairs={{0,4},{4,0},{1,5},{5,1},{2,6},{6,2},{3,7},{7,3},{8,12},{12,8},{9,1... | collective-permute-start | bytes 442376 | tf_op jit(solution)/shard_map/ppermute | solution.py:32
  3.4 9.2 %collective-permute-start.7 = (bf16[2,2,18,8,128]{4,3,2,1,0:T(8,128)(2,1)S(1)}, bf16[2,2,18,8,128]{4,3,2,1,0:T(8,128)(2,1)S(1)}, u32[]{:S(2)}, u32[]{:S(2)}) collective-permute-start(bf16[2,2,18,8,128]{4,3,2,1,0:T(8,128)(2,1)S(1)} %pad_maximum_fusion.2), channel_id=1, source_target_pairs={{0,1},{1,2},{2,3},{3,0},{4,5},{5,6},{6,7},{7,4},{8,9},{9,10},{10,1... | collective-permute-start | bytes 442376 | tf_op jit(solution)/shard_map/ppermute | solution.py:32
  6.1 8.3 %collective-permute-start.5 = (bf16[2,2,18,8,128]{4,3,2,1,0:T(8,128)(2,1)S(1)}, bf16[2,2,18,8,128]{4,3,2,1,0:T(8,128)(2,1)S(1)}, u32[]{:S(2)}, u32[]{:S(2)}) collective-permute-start(bf16[2,2,18,8,128]{4,3,2,1,0:T(8,128)(2,1)S(1)} %pad_maximum_fusion), channel_id=1, source_target_pairs={{0,8},{8,16},{16,24},{24,0},{1,9},{9,17},{17,25},{25,1},{2,10},{10... | collective-permute-start | bytes 442376 | tf_op jit(solution)/shard_map/ppermute | solution.py:32
  7.6 9.1 %collective-permute-start = (f32[6,8,128]{2,1,0:T(8,128)S(1)}, f32[6,8,128]{2,1,0:T(8,128)S(1)}, u32[]{:S(2)}, u32[]{:S(2)}) collective-permute-start(f32[6,8,128]{2,1,0:T(8,128)S(1)} %bitcast.17), channel_id=1, source_target_pairs={{0,24},{8,0},{16,8},{24,16},{1,25},{9,1},{17,9},{25,17},{2,26},{10... | collective-permute-start | bytes 73736 | tf_op jit(solution)/shard_map/ppermute | solution.py:32
  9.1 7.6 %collective-permute-start.1 = (f32[6,8,128]{2,1,0:T(8,128)S(1)}, f32[6,8,128]{2,1,0:T(8,128)S(1)}, u32[]{:S(2)}, u32[]{:S(2)}) collective-permute-start(f32[6,8,128]{2,1,0:T(8,128)S(1)} %bitcast.18), channel_id=1, source_target_pairs={{0,8},{8,16},{16,24},{24,0},{1,9},{9,17},{17,25},{25,1},{2,10},{10... | collective-permute-start | bytes 73736 | tf_op jit(solution)/shard_map/ppermute | solution.py:32
  9.7 7.1 %collective-permute-start.2 = (f32[6,8,128]{2,1,0:T(8,128)S(1)}, f32[6,8,128]{2,1,0:T(8,128)S(1)}, u32[]{:S(2)}, u32[]{:S(2)}) collective-permute-start(f32[6,8,128]{2,1,0:T(8,128)S(1)} %bitcast.19), channel_id=1, source_target_pairs={{0,4},{4,0},{1,5},{5,1},{2,6},{6,2},{3,7},{7,3},{8,12},{12,8},{9,1... | collective-permute-start | bytes 73736 | tf_op jit(solution)/shard_map/ppermute | solution.py:32
  14.3 5.6 %collective-permute-start.4 = (f32[6,8,128]{2,1,0:T(8,128)S(1)}, f32[6,8,128]{2,1,0:T(8,128)S(1)}, u32[]{:S(2)}, u32[]{:S(2)}) collective-permute-start(f32[6,8,128]{2,1,0:T(8,128)S(1)} %bitcast.21), channel_id=1, source_target_pairs={{0,1},{1,2},{2,3},{3,0},{4,5},{5,6},{6,7},{7,4},{8,9},{9,10},{10,1... | collective-permute-start | bytes 73736 | tf_op jit(solution)/shard_map/ppermute | solution.py:32
  20.3 5.7 %collective-permute-start.12 = (f32[6,8,128]{2,1,0:T(8,128)S(1)}, f32[6,8,128]{2,1,0:T(8,128)S(1)}, u32[]{:S(2)}, u32[]{:S(2)}) collective-permute-start(f32[6,8,128]{2,1,0:T(8,128)S(1)} %shard_map.51.field_ref), channel_id=1, source_target_pairs={{0,1},{1,2},{2,3},{3,0},{4,5},{5,6},{6,7},{7,4},{8,9},{9,10},{10,1... | collective-permute-start | bytes 73736 | tf_op jit(solution)/shard_map/ppermute | solution.py:32
  24.8 4.7 %collective-permute-start.9 = (f32[6,8,128]{2,1,0:T(8,128)S(1)}, f32[6,8,128]{2,1,0:T(8,128)S(1)}, u32[]{:S(2)}, u32[]{:S(2)}) collective-permute-start(f32[6,8,128]{2,1,0:T(8,128)S(1)} %shard_map.51.field_ref), channel_id=1, source_target_pairs={{0,8},{8,16},{16,24},{24,0},{1,9},{9,17},{17,25},{25,1},{2,10},{10... | collective-permute-start | bytes 73736 | tf_op jit(solution)/shard_map/ppermute | solution.py:32
  29.8 4.8 %collective-permute-start.14 = (f32[6,8,128]{2,1,0:T(8,128)S(1)}, f32[6,8,128]{2,1,0:T(8,128)S(1)}, u32[]{:S(2)}, u32[]{:S(2)}) collective-permute-start(f32[6,8,128]{2,1,0:T(8,128)S(1)} %shard_map.52.field_ref.start_ref.refs_1_), channel_id=1, source_target_pairs={{0,8},{8,16},{16,24},{24,0},{1,9},{9,17},{17,25},{25,1},{2,10},{10... | collective-permute-start | bytes 73736 | tf_op jit(solution)/shard_map/ppermute | solution.py:32
  33.7 5.6 %collective-permute-start.17 = (f32[6,8,128]{2,1,0:T(8,128)S(1)}, f32[6,8,128]{2,1,0:T(8,128)S(1)}, u32[]{:S(2)}, u32[]{:S(2)}) collective-permute-start(f32[6,8,128]{2,1,0:T(8,128)S(1)} %shard_map.52.field_ref.start_ref.refs_1_), channel_id=1, source_target_pairs={{0,1},{1,2},{2,3},{3,0},{4,5},{5,6},{6,7},{7,4},{8,9},{9,10},{10,1... | collective-permute-start | bytes 73736 | tf_op jit(solution)/shard_map/ppermute | solution.py:32
  41.7 5.6 %collective-permute-start.22 = (f32[6,8,128]{2,1,0:T(8,128)S(1)}, f32[6,8,128]{2,1,0:T(8,128)S(1)}, u32[]{:S(2)}, u32[]{:S(2)}) collective-permute-start(f32[6,8,128]{2,1,0:T(8,128)S(1)} %shard_map.53.field_ref), channel_id=1, source_target_pairs={{0,1},{1,2},{2,3},{3,0},{4,5},{5,6},{6,7},{7,4},{8,9},{9,10},{10,1... | collective-permute-start | bytes 73736 | tf_op jit(solution)/shard_map/ppermute | solution.py:32
  58.9 4.7 %collective-permute-start.24 = (f32[6,8,128]{2,1,0:T(8,128)S(1)}, f32[6,8,128]{2,1,0:T(8,128)S(1)}, u32[]{:S(2)}, u32[]{:S(2)}) collective-permute-start(f32[6,8,128]{2,1,0:T(8,128)S(1)} %get-tuple-element.28.field_ref.start_ref.refs_3_), channel_id=1, source_target_pairs={{0,8},{8,16},{16,24},{24,0},{1,9},{9,17},{17,25},{25,1},{2,10},{10... | collective-permute-start | bytes 73736 | tf_op jit(solution)/shard_map/ppermute | solution.py:32
  61.4 5.6 %collective-permute-start.27 = (f32[6,8,128]{2,1,0:T(8,128)S(1)}, f32[6,8,128]{2,1,0:T(8,128)S(1)}, u32[]{:S(2)}, u32[]{:S(2)}) collective-permute-start(f32[6,8,128]{2,1,0:T(8,128)S(1)} %get-tuple-element.28.field_ref.start_ref.refs_3_), channel_id=1, source_target_pairs={{0,1},{1,2},{2,3},{3,0},{4,5},{5,6},{6,7},{7,4},{8,9},{9,10},{10,1... | collective-permute-start | bytes 73736 | tf_op jit(solution)/shard_map/ppermute | solution.py:32
  69.5 5.6 %collective-permute-start.32 = (f32[6,8,128]{2,1,0:T(8,128)S(1)}, f32[6,8,128]{2,1,0:T(8,128)S(1)}, u32[]{:S(2)}, u32[]{:S(2)}) collective-permute-start(f32[6,8,128]{2,1,0:T(8,128)S(1)} %shard_map.57.field_ref), channel_id=1, source_target_pairs={{0,1},{1,2},{2,3},{3,0},{4,5},{5,6},{6,7},{7,4},{8,9},{9,10},{10,1... | collective-permute-start | bytes 73736 | tf_op jit(solution)/shard_map/ppermute | solution.py:32
  77.8 4.7 %collective-permute-start.34 = (f32[6,8,128]{2,1,0:T(8,128)S(1)}, f32[6,8,128]{2,1,0:T(8,128)S(1)}, u32[]{:S(2)}, u32[]{:S(2)}) collective-permute-start(f32[6,8,128]{2,1,0:T(8,128)S(1)} %shard_map.58.field_ref.start_ref.refs_4_), channel_id=1, source_target_pairs={{0,8},{8,16},{16,24},{24,0},{1,9},{9,17},{17,25},{25,1},{2,10},{10... | collective-permute-start | bytes 73736 | tf_op jit(solution)/shard_map/ppermute | solution.py:32
  78.1 5.6 %collective-permute-start.37 = (f32[6,8,128]{2,1,0:T(8,128)S(1)}, f32[6,8,128]{2,1,0:T(8,128)S(1)}, u32[]{:S(2)}, u32[]{:S(2)}) collective-permute-start(f32[6,8,128]{2,1,0:T(8,128)S(1)} %shard_map.58.field_ref.start_ref.refs_4_), channel_id=1, source_target_pairs={{0,1},{1,2},{2,3},{3,0},{4,5},{5,6},{6,7},{7,4},{8,9},{9,10},{10,1... | collective-permute-start | bytes 73736 | tf_op jit(solution)/shard_map/ppermute | solution.py:32
  84.0 5.0 %collective-permute-start.38 = (f32[6,8,128]{2,1,0:T(8,128)S(1)}, f32[6,8,128]{2,1,0:T(8,128)S(1)}, u32[]{:S(2)}, u32[]{:S(2)}) collective-permute-start(f32[6,8,128]{2,1,0:T(8,128)S(1)} %shard_map.59.field_ref), channel_id=1, source_target_pairs={{0,24},{8,0},{16,8},{24,16},{1,25},{9,1},{17,9},{25,17},{2,26},{10... | collective-permute-start | bytes 73736 | tf_op jit(solution)/shard_map/ppermute | solution.py:32
  87.0 5.6 %collective-permute-start.42 = (f32[6,8,128]{2,1,0:T(8,128)S(1)}, f32[6,8,128]{2,1,0:T(8,128)S(1)}, u32[]{:S(2)}, u32[]{:S(2)}) collective-permute-start(f32[6,8,128]{2,1,0:T(8,128)S(1)} %shard_map.59.field_ref), channel_id=1, source_target_pairs={{0,1},{1,2},{2,3},{3,0},{4,5},{5,6},{6,7},{7,4},{8,9},{9,10},{10,1... | collective-permute-start | bytes 73736 | tf_op jit(solution)/shard_map/ppermute | solution.py:32
  107.9 5.6 %collective-permute-start.47 = (f32[6,8,128]{2,1,0:T(8,128)S(1)}, f32[6,8,128]{2,1,0:T(8,128)S(1)}, u32[]{:S(2)}, u32[]{:S(2)}) collective-permute-start(f32[6,8,128]{2,1,0:T(8,128)S(1)} %get-tuple-element.34.field_ref.start_ref.refs_3_), channel_id=1, source_target_pairs={{0,1},{1,2},{2,3},{3,0},{4,5},{5,6},{6,7},{7,4},{8,9},{9,10},{10,1... | collective-permute-start | bytes 73736 | tf_op jit(solution)/shard_map/ppermute | solution.py:32
  116.0 5.6 %collective-permute-start.52 = (f32[6,8,128]{2,1,0:T(8,128)S(1)}, f32[6,8,128]{2,1,0:T(8,128)S(1)}, u32[]{:S(2)}, u32[]{:S(2)}) collective-permute-start(f32[6,8,128]{2,1,0:T(8,128)S(1)} %shard_map.63.field_ref), channel_id=1, source_target_pairs={{0,1},{1,2},{2,3},{3,0},{4,5},{5,6},{6,7},{7,4},{8,9},{9,10},{10,1... | collective-permute-start | bytes 73736 | tf_op jit(solution)/shard_map/ppermute | solution.py:32
  124.6 5.6 %collective-permute-start.57 = (f32[6,8,128]{2,1,0:T(8,128)S(1)}, f32[6,8,128]{2,1,0:T(8,128)S(1)}, u32[]{:S(2)}, u32[]{:S(2)}) collective-permute-start(f32[6,8,128]{2,1,0:T(8,128)S(1)} %shard_map.64.field_ref.start_ref.refs_4_), channel_id=1, source_target_pairs={{0,1},{1,2},{2,3},{3,0},{4,5},{5,6},{6,7},{7,4},{8,9},{9,10},{10,1... | collective-permute-start | bytes 73736 | tf_op jit(solution)/shard_map/ppermute | solution.py:32
  130.4 5.0 %collective-permute-start.58 = (f32[6,8,128]{2,1,0:T(8,128)S(1)}, f32[6,8,128]{2,1,0:T(8,128)S(1)}, u32[]{:S(2)}, u32[]{:S(2)}) collective-permute-start(f32[6,8,128]{2,1,0:T(8,128)S(1)} %shard_map.65.field_ref), channel_id=1, source_target_pairs={{0,24},{8,0},{16,8},{24,16},{1,25},{9,1},{17,9},{25,17},{2,26},{10... | collective-permute-start | bytes 73736 | tf_op jit(solution)/shard_map/ppermute | solution.py:32
  133.4 5.6 %collective-permute-start.62 = (f32[6,8,128]{2,1,0:T(8,128)S(1)}, f32[6,8,128]{2,1,0:T(8,128)S(1)}, u32[]{:S(2)}, u32[]{:S(2)}) collective-permute-start(f32[6,8,128]{2,1,0:T(8,128)S(1)} %shard_map.65.field_ref), channel_id=1, source_target_pairs={{0,1},{1,2},{2,3},{3,0},{4,5},{5,6},{6,7},{7,4},{8,9},{9,10},{10,1... | collective-permute-start | bytes 73736 | tf_op jit(solution)/shard_map/ppermute | solution.py:32
  154.3 5.6 %collective-permute-start.67 = (f32[6,8,128]{2,1,0:T(8,128)S(1)}, f32[6,8,128]{2,1,0:T(8,128)S(1)}, u32[]{:S(2)}, u32[]{:S(2)}) collective-permute-start(f32[6,8,128]{2,1,0:T(8,128)S(1)} %get-tuple-element.40.field_ref.start_ref.refs_3_), channel_id=1, source_target_pairs={{0,1},{1,2},{2,3},{3,0},{4,5},{5,6},{6,7},{7,4},{8,9},{9,10},{10,1... | collective-permute-start | bytes 73736 | tf_op jit(solution)/shard_map/ppermute | solution.py:32
  162.4 5.6 %collective-permute-start.72 = (f32[6,8,128]{2,1,0:T(8,128)S(1)}, f32[6,8,128]{2,1,0:T(8,128)S(1)}, u32[]{:S(2)}, u32[]{:S(2)}) collective-permute-start(f32[6,8,128]{2,1,0:T(8,128)S(1)} %shard_map.69.field_ref), channel_id=1, source_target_pairs={{0,1},{1,2},{2,3},{3,0},{4,5},{5,6},{6,7},{7,4},{8,9},{9,10},{10,1... | collective-permute-start | bytes 73736 | tf_op jit(solution)/shard_map/ppermute | solution.py:32
  171.0 5.6 %collective-permute-start.77 = (f32[6,8,128]{2,1,0:T(8,128)S(1)}, f32[6,8,128]{2,1,0:T(8,128)S(1)}, u32[]{:S(2)}, u32[]{:S(2)}) collective-permute-start(f32[6,8,128]{2,1,0:T(8,128)S(1)} %shard_map.70.field_ref.start_ref.refs_4_), channel_id=1, source_target_pairs={{0,1},{1,2},{2,3},{3,0},{4,5},{5,6},{6,7},{7,4},{8,9},{9,10},{10,1... | collective-permute-start | bytes 73736 | tf_op jit(solution)/shard_map/ppermute | solution.py:32
  176.8 5.0 %collective-permute-start.78 = (f32[6,8,128]{2,1,0:T(8,128)S(1)}, f32[6,8,128]{2,1,0:T(8,128)S(1)}, u32[]{:S(2)}, u32[]{:S(2)}) collective-permute-start(f32[6,8,128]{2,1,0:T(8,128)S(1)} %shard_map.71.field_ref), channel_id=1, source_target_pairs={{0,24},{8,0},{16,8},{24,16},{1,25},{9,1},{17,9},{25,17},{2,26},{10... | collective-permute-start | bytes 73736 | tf_op jit(solution)/shard_map/ppermute | solution.py:32
  179.8 5.6 %collective-permute-start.82 = (f32[6,8,128]{2,1,0:T(8,128)S(1)}, f32[6,8,128]{2,1,0:T(8,128)S(1)}, u32[]{:S(2)}, u32[]{:S(2)}) collective-permute-start(f32[6,8,128]{2,1,0:T(8,128)S(1)} %shard_map.71.field_ref), channel_id=1, source_target_pairs={{0,1},{1,2},{2,3},{3,0},{4,5},{5,6},{6,7},{7,4},{8,9},{9,10},{10,1... | collective-permute-start | bytes 73736 | tf_op jit(solution)/shard_map/ppermute | solution.py:32
  198.8 4.9 %collective-permute-start.84 = (f32[6,8,128]{2,1,0:T(8,128)}, f32[6,8,128]{2,1,0:T(8,128)S(1)}, u32[]{:S(2)}, u32[]{:S(2)}) collective-permute-start(f32[6,8,128]{2,1,0:T(8,128)} %get-tuple-element.43.field_ref.start_ref), channel_id=1, source_target_pairs={{0,8},{8,16},{16,24},{24,0},{1,9},{9,17},{17,25},{25,1},{2,10},{10... | collective-permute-start | bytes 73736 | tf_op jit(solution)/shard_map/ppermute | solution.py:32
  201.3 5.8 %collective-permute-start.87 = (f32[6,8,128]{2,1,0:T(8,128)}, f32[6,8,128]{2,1,0:T(8,128)S(1)}, u32[]{:S(2)}, u32[]{:S(2)}) collective-permute-start(f32[6,8,128]{2,1,0:T(8,128)} %get-tuple-element.43.field_ref.start_ref), channel_id=1, source_target_pairs={{0,1},{1,2},{2,3},{3,0},{4,5},{5,6},{6,7},{7,4},{8,9},{9,10},{10,1... | collective-permute-start | bytes 73736 | tf_op jit(solution)/shard_map/ppermute | solution.py:32
  210.3 5.6 %collective-permute-start.92 = (f32[6,8,128]{2,1,0:T(8,128)S(1)}, f32[6,8,128]{2,1,0:T(8,128)S(1)}, u32[]{:S(2)}, u32[]{:S(2)}) collective-permute-start(f32[6,8,128]{2,1,0:T(8,128)S(1)} %shard_map.75.field_ref), channel_id=1, source_target_pairs={{0,1},{1,2},{2,3},{3,0},{4,5},{5,6},{6,7},{7,4},{8,9},{9,10},{10,1... | collective-permute-start | bytes 73736 | tf_op jit(solution)/shard_map/ppermute | solution.py:32
  (64 other events, 275.2 us)

commit v2 on v1

v2 whole, which is shorter than its diff:
```python
import jax
import jax.numpy as jnp
from jax import lax
from jax.experimental import pallas as pl
from jax.experimental.pallas import tpu as pltpu
from jax.sharding import PartitionSpec as P

NX = 32
ITERS = 8
FIRST = 2

mass_squared = 0.1
SCALE = 1.0 / 16.0

VMEM = pl.BlockSpec(memory_space=pltpu.VMEM)
PARAMS = pltpu.CompilerParams(vmem_limit_bytes=4 * 2**20)
AXES = ("ta", "gz", "gy")


def on_core(body, outs, *args):
    return pl.pallas_call(
        body,
        out_shape=tuple(jax.ShapeDtypeStruct(shape, jnp.float32) for shape in outs),
        in_specs=[VMEM] * len(args),
        out_specs=tuple(VMEM for _ in outs),
        compiler_params=PARAMS,
    )(*args)


def passed_along(shard, axis, by):
    size = lax.axis_size(axis)
    return lax.ppermute(shard, axis, [(i, (i + by) % size) for i in range(size)])


def swapped(shard, axis, odd):
    size = lax.axis_size(axis)
    assert size % 2 == 0
    ahead = [(i, (i + 1) % size) for i in range(odd, size, 2)]
    return lax.ppermute(shard, axis, ahead + [(j, i) for i, j in ahead])


def rolled(tile, shift, axis):
    shift = shift % tile.shape[axis]
    return pltpu.roll(tile, shift, axis) if shift else tile


class Shifts:
    def __init__(self, rows, depth, width):
        self.rows, self.depth, self.width = (rows, depth, width)
        self.shape = (rows * depth, width)
        sub = lax.broadcasted_iota(jnp.int32, self.shape, 0)
        self.lane = lax.broadcasted_iota(jnp.int32, self.shape, 1)
        self.row = sub // depth
        self.plane = sub % depth
        self.x = self.lane % NX
        self.odd = (self.plane + self.lane // NX + self.x) % 2 == 1

    def select(self, dst):
        return self.odd if dst == 0 else jnp.logical_not(self.odd)

    def t_rows(self, own, other, by):
        if by == 0:
            return own
        near = self.row >= by if by > 0 else self.row < self.rows + by
        return rolled(jnp.where(near, own, other), -by * self.depth, 0)

    def t(self, own, other, by, dst):
        sel = self.select(dst)
        half = {1: (1, 0), 3: (2, 1), -1: (0, -1), -3: (-1, -2)}[by]
        return jnp.where(sel, self.t_rows(own, other, half[0]), self.t_rows(own, other, half[1]))

    def z(self, own, other, by):
        near = self.plane < self.depth - by if by > 0 else self.plane >= -by
        wrap = self.depth - by if by > 0 else -self.depth - by
        return jnp.where(near, rolled(own, -by, 0), rolled(other, wrap, 0))

    def y(self, own, other, by):
        lanes = by * NX
        near = self.lane >= lanes if by > 0 else self.lane < self.width + lanes
        return rolled(jnp.where(near, own, other), -lanes, 1)

    def x_(self, own, by):
        near = self.x < NX - by if by > 0 else self.x >= -by
        wrap = NX - by if by > 0 else -NX - by
        return jnp.where(near, rolled(own, -by, 1), rolled(own, wrap, 1))

    def hop(self, own, other, mu, by, dst):
        if mu == 0:
            return self.t(own, other, by, dst)
        if mu == 1:
            return self.z(own, other, by)
        if mu == 2:
            return self.y(own, other, by)
        return self.x_(own, by)


HOPS = tuple((mu, by) for mu in range(4) for by in (1, 3, -1, -3))


def link_table(fat, long, near, dims, dst):
    rows, depth, width = dims
    tile = (rows * depth, width)

    def body(fat_ref, long_ref, t_ref, z_ref, y_ref, out):
        shifts = Shifts(rows, depth, width)
        lows = (t_ref, z_ref, y_ref)

        def entry(i, carry):
            flip = 3 * (i % 3) + i // 3
            for k, (mu, by) in enumerate(HOPS):
                kind = 0 if abs(by) == 1 else 1
                ref = (fat_ref, long_ref)[kind]
                for part in range(2):
                    if by > 0:
                        value = ref[dst, mu, 9 * part + i].astype(jnp.float32)
                        out[18 * k + 9 * part + i] = value
                    else:
                        own = ref[1 - dst, mu, 9 * part + i].astype(jnp.float32)
                        other = own
                        if mu < 3:
                            other = lows[mu][kind, 1 - dst, 9 * part + i].astype(jnp.float32)
                        value = shifts.hop(own, other, mu, by, dst)
                        out[18 * k + 9 * part + flip] = value if part else -value
            return carry

        lax.fori_loop(0, 9, entry, 0)

    return on_core(body, [(18 * len(HOPS),) + tile], fat, long, *near)[0]


def hopping_sum(shifts, field, near, table, dst):
    flags = near[-1]
    total = [None] * 6
    for mu in range(4):
        ahead = behind = [None] * 6
        if mu < 3:
            one, two = (near[2 * mu], near[2 * mu + 1])
            if one is two:
                ahead = behind = [one[c] for c in range(6)]
            else:
                even = flags[mu] > 0.5
                pairs = [(one[c], two[c]) for c in range(6)]
                ahead = [jnp.where(even, u, v) for u, v in pairs]
                behind = [jnp.where(even, v, u) for u, v in pairs]
        for k, (axis, by) in enumerate(HOPS):
            if axis != mu:
                continue
            other = ahead if by > 0 else behind
            hopped = [shifts.hop(field[c], other[c], mu, by, dst) for c in range(6)]
            for a in range(3):
                re = im = None
                for b in range(3):
                    lre = table[18 * k + 3 * a + b]
                    lim = table[18 * k + 9 + 3 * a + b]
                    vre, vim = (hopped[b], hopped[3 + b])
                    x, y = (lre * vre - lim * vim, lre * vim + lim * vre)
                    re = x if re is None else re + x
                    im = y if im is None else im + y
                total[a] = re if total[a] is None else total[a] + re
                total[3 + a] = im if total[3 + a] is None else total[3 + a] + im
    return total


def axis_sizes():
    return tuple(lax.axis_size(axis) for axis in AXES)


def swaps_of(sizes):
    return tuple(
        (mu, odd) for odd in (1, 0) for mu in (2, 0, 1) if odd == 0 or sizes[mu] > 2
    )


def neighbours(field):
    return tuple(swapped(field, AXES[mu], odd) for mu, odd in swaps_of(axis_sizes()))


def spread(refs, sizes):
    keys = swaps_of(sizes)
    got = dict(zip(keys, refs))
    near = [got.get((mu, odd), got[mu, 0]) for mu in range(3) for odd in (0, 1)]
    return near, list(refs[len(keys) :])


def odd_from_even(field, table, flags, dims):
    sizes = axis_sizes()

    def body(field_ref, table_ref, flags_ref, *refs):
        near, (out,) = spread(refs, sizes)
        shifts = Shifts(*dims)
        for c, value in enumerate(hopping_sum(shifts, field_ref, near + [flags_ref], table_ref, 1)):
            out[c] = value

    return on_core(body, [field.shape], field, table, flags, *neighbours(field))[0]


def even_from_odd(field, start, table, flags, dims, finish, *extra):
    sizes = axis_sizes()

    def body(field_ref, start_ref, table_ref, flags_ref, *refs):
        near, rest = spread(refs, sizes)
        more, out = (rest[:-1], rest[-1])
        shifts = Shifts(*dims)
        for c, value in enumerate(hopping_sum(shifts, field_ref, near + [flags_ref], table_ref, 0)):
            out[c] = finish(c, mass_squared * start_ref[c] - value, start_ref, more)

    near = neighbours(field)
    return on_core(body, [field.shape], field, start, table, flags, *near, *extra)[0]


def pairs_of(count):
    return tuple((i, j) for i in range(count) for j in range(i, count))


def gram_parts(basis, copies):
    parts, width = (basis[0].shape[0], 128)

    def body(*refs):
        out = refs[-1]
        lane = lax.broadcasted_iota(jnp.int32, (8, width), 1)
        row = lax.broadcasted_iota(jnp.int32, (8, width), 0)
        packed = jnp.zeros((8, width), jnp.float32)
        for n, (i, j) in enumerate(pairs_of(len(basis))):
            tile = refs[i][0] * refs[j][0]
            for c in range(1, parts):
                tile = tile + refs[i][c] * refs[j][c]
            value = jnp.sum(jnp.sum(tile, axis=0, keepdims=True), axis=1, keepdims=True)
            packed = jnp.where(jnp.logical_and(row == n % 8, lane == n // 8), value, packed)
        for k in range(copies):
            out[k] = packed

    return on_core(body, [(copies, 8, width)], *basis)[0]


def add(a, b):
    return b if a is None else a if b is None else a + b


def times(s, vec):
    return {i: s * v for i, v in vec.items()}


def plus(u, v):
    return {i: add(u.get(i), v.get(i)) for i in sorted(set(u) | set(v))}


def iterations(count, gram, applied, residual, direction, norm, gain):
    def dot(u, v):
        out = None
        for i, a in u.items():
            part = None
            for j, b in v.items():
                part = add(part, gram[i, j] * b)
            out = add(out, a * part)
        return out

    log = []
    for step in range(count):
        image = applied(direction)
        alpha = norm / dot(direction, image)
        gain = plus(gain, times(alpha, direction))
        residual = plus(residual, times(-alpha, image))
        last = direction
        if step + 1 < count:
            norm_next = dot(residual, residual)
            log.append((alpha, norm_next / norm, norm))
            direction = plus(residual, times(norm_next / norm, direction))
            norm = norm_next
        else:
            log.append((alpha, None, norm))
    return gain, residual, last, log


def gram_of(sums_ref, count, tile):
    total = sums_ref[0]
    for k in range(1, sums_ref.shape[0]):
        total = total + sums_ref[k]
    gram = {}
    for n, (i, j) in enumerate(pairs_of(count)):
        value = jnp.broadcast_to(total[n % 8 : n % 8 + 1, n // 8 : n // 8 + 1], tile)
        gram[i, j] = gram[j, i] = value
    return gram


def first_update(sums, basis):
    shape = basis[0].shape
    tile = shape[1:]

    def body(sums_ref, v0, v1, v2, state_out, r_out):
        gram = gram_of(sums_ref, 3, tile)

        def applied(u):
            return {i + 1: a * (1.0 / SCALE) for i, a in u.items()}

        start = {0: jnp.ones(tile, jnp.float32)}
        gain, residual, direction, log = iterations(
            FIRST, gram, applied, start, start, gram[0, 0], {}
        )
        (alpha0, beta0, _), (alpha1, _, norm) = log
        centre = 1.0 / alpha1 + beta0 / alpha0
        spread_ = jnp.maximum(jnp.sqrt(jnp.maximum(beta0, 0.0)) / alpha0, 1e-3 * centre)
        kept = (
            norm, direction[0], direction[1], gain[0], gain[1],
            residual[0], residual[1], residual[2], centre, spread_, 1.0 / spread_,
        )
        for n, value in enumerate(kept):
            state_out[n] = value
        for c in range(shape[0]):
            r_out[c] = residual[0] * v0[c] + residual[1] * v1[c] + residual[2] * v2[c]

    return on_core(body, [(STATE,) + tile, shape], sums, *basis)


STATE = 11
CENTRE, WIDTH, INVERSE = (8, 9, 10)


def last_update(sums, state, basis):
    shape = basis[0].shape
    tile = shape[1:]
    count = len(basis)

    def body(sums_ref, state_ref, *refs):
        vectors, x_out = (refs[:-1], refs[-1])
        gram = gram_of(sums_ref, count, tile)
        kept = [state_ref[n] for n in range(STATE)]
        norm_before, p0, p1, g0, g1, c0, c1, c2, centre, width, _ = kept
        share = (1.0 / SCALE) / c2
        second = {0: -share * c0, 1: -share * c1, 2: share}

        def applied(u):
            out = {}
            for i, a in u.items():
                if i == 0:
                    out = plus(out, {1: a * (1.0 / SCALE)})
                elif i == 1:
                    out = plus(out, times(a, second))
                else:
                    wide = a * width
                    out = plus(out, {i: a * centre, i + 1: wide})
                    if i > 2:
                        out = plus(out, {i - 1: wide})
            return out

        one = jnp.ones(tile, jnp.float32)
        norm = gram[2, 2]
        ratio = norm / norm_before
        direction = {0: ratio * p0, 1: ratio * p1, 2: one}
        gain, _, _, _ = iterations(
            ITERS - FIRST, gram, applied, {2: one}, direction, norm, {0: g0, 1: g1}
        )
        for c in range(shape[0]):
            x_out[c] = sum(s * vectors[i][c] for i, s in gain.items())

    return on_core(body, [shape], sums, state, *basis)[0]


def per_device(source, fat_links, long_links):
    rows, depth, width = source.shape[2:]
    dims = (rows, depth, width)
    tile = (rows * depth, width)
    field = source.reshape((6,) + tile)
    fat = fat_links.reshape((2, 4, 18) + tile)
    long = long_links.reshape((2, 4, 18) + tile)
    near = [
        passed_along(jnp.stack([fat[:, mu], long[:, mu]]), axis, 1)
        for mu, axis in enumerate(AXES)
    ]
    odd_table = link_table(fat, long, near, dims, 1)
    even_table = link_table(fat, long, near, dims, 0)
    even = jnp.stack([lax.axis_index(axis) % 2 == 0 for axis in AXES])
    flags = jnp.broadcast_to(even.astype(jnp.float32)[:, None, None], (len(AXES),) + tile)

    devices = 1
    for size in axis_sizes():
        devices *= size

    def image(vector, finish, *extra):
        odd = odd_from_even(vector, odd_table, flags, dims)
        return even_from_odd(odd, vector, even_table, flags, dims, finish, *extra)

    def summed(basis):
        return lax.all_to_all(gram_parts(basis, devices), AXES, 0, 0, tiled=True)

    def scaled(c, value, vector, more):
        return SCALE * value

    def shifted(c, value, vector, more):
        state = more[0]
        value = (value - state[CENTRE] * vector[c]) * state[INVERSE]
        return value - more[1][c] if len(more) > 1 else value

    def remaining(c, value, vector, more):
        return more[0][c] - value

    basis = [field]
    for _ in range(FIRST):
        basis.append(image(basis[-1], scaled))
    state, residual = first_update(summed(basis), basis)
    basis = basis[:FIRST] + [residual]
    for step in range(ITERS - FIRST):
        basis.append(image(basis[-1], shifted, state, *([basis[-2]] if step else [])))
    solution = last_update(summed(basis), state, basis)
    true = image(solution, remaining, field)
    return (solution.reshape(source.shape), true.reshape(source.shape))


def solution(mesh):
    in_specs = (
        P(None, None, "ta", "gz", "gy"),
        P(None, None, None, None, None, "ta", "gz", "gy"),
        P(None, None, None, None, None, "ta", "gz", "gy"),
    )
    out_specs = (P(None, None, "ta", "gz", "gy"), P(None, None, "ta", "gz", "gy"))
    return jax.shard_map(
        per_device, mesh=mesh, in_specs=in_specs, out_specs=out_specs, check_vma=False
    )
```

time: 217 us -> 179 us (0.82)
  waiting for transfers between devices: 76.5 us -> 47.3 us
  blocking collectives: 44.6 us -> 20.9 us
  starting transfers between devices: 83.9 us -> 98.3 us
    ppermute x0 -> x90, starting transfers between devices: none -> 93.6 us  [swapped(): return lax.ppermute(shard, axis, ahead + [(j, i) for i, j in ahead])]
    ppermute x93 -> x3, starting transfers between devices: 83.9 us -> 4.72 us  [passed_along(): lax.ppermute(shard, axis, [(i, (i + by) % size) for i in range(size)])]
    ppermute x93 -> x3, waiting for transfers between devices: 76.5 us -> 0.84 us  [passed_along(): lax.ppermute(shard, axis, [(i, (i + by) % size) for i in range(size)])]
    ppermute x0 -> x90, waiting for transfers between devices: none -> 46.5 us  [swapped(): return lax.ppermute(shard, axis, ahead + [(j, i) for i, j in ahead])]
    all_to_all x4 -> x2, blocking collectives: 44.6 us -> 20.9 us  [summed(): return lax.all_to_all(gram_parts(basis, devices), AXES, 0, 0, tiled=True)]
    pallas_call x27 -> x24, Pallas kernels: 7.78 us -> 7.68 us  [on_core(): pl.pallas_call(body, out_shape=tuple((jax.ShapeDtypeStruct(shape, jnp.flo...]
  transfers between devices with their start and end apart: 93 -> 93, of which waited for: 43 -> 47; matrix products, arithmetic and copies ran while one was open for 0% -> 0% of each run, Pallas kernels for 1% -> 1%
where the time goes in v2:
time: 179 us; the launch traced here: 178 us
  starting transfers between devices  98.3 us (55%)
  waiting for transfers between devices  47.3 us (26%)
  blocking collectives  20.9 us (12%)
  Pallas kernels  7.68 us (4%)
  local copies, waits for them, and re-layouts  3.02 us (2%)
    ppermute x90, starting transfers between devices, swapped(): return lax.ppermute(shard, axis, ahead + [(j, i) for i, j in ahead])  93.6 us
    ppermute x90, waiting for transfers between devices, swapped(): return lax.ppermute(shard, axis, ahead + [(j, i) for i, j in ahead])  46.5 us
    all_to_all x2, blocking collectives, summed(): return lax.all_to_all(gram_parts(basis, devices), AXES, 0, 0, tiled=True)  20.9 us
    pallas_call x24, Pallas kernels, on_core(): pl.pallas_call(body, out_shape=tuple((jax.ShapeDtypeStruct(shape, jnp.flo...  7.68 us
    ppermute x3, starting transfers between devices, passed_along(): lax.ppermute(shard, axis, [(i, (i + by) % size) for i in range(size)])  4.72 us
  transfers between devices with their start and end apart: 93, of which 47 were waited for; matrix products, arithmetic and copies ran while one was open for 0% of the time, Pallas kernels for 1%

profile of v2, /device:TPU:0, one launch (start us, length us, event | category | flops | bytes accessed | tf_op | source)
XLA Modules:
  0.0 178.3 jit_solution(6925603877144259810)
XLA Ops:
  2.8 3.0 %collective-permute-start = (bf16[2,2,18,8,128]{4,3,2,1,0:T(8,128)(2,1)S(1)}, bf16[2,2,18,8,128]{4,3,2,1,0:T(8,128)(2,1)S(1)}, u32[]{:S(2)}, u32[]{:S(2)}) collective-permute-start(bf16[2,2,18,8,128]{4,3,2,1,0:T(8,128)(2,1)S(1)} %pad_maximum_fusion), channel_id=1, source_target_pairs={{0,8},{8,16},{16,24},{24,0},{1,9},{9,17},{17,25},{25,1},{2,10},{10... | collective-permute-start | bytes 442376 | tf_op jit(solution)/shard_map/ppermute | solution.py:32
  6.0 1.6 collective-permute-start.2
  7.6 2.2 %collective-permute-start.3 = (f32[6,8,128]{2,1,0:T(8,128)S(1)}, f32[6,8,128]{2,1,0:T(8,128)S(1)}, u32[]{:S(2)}, u32[]{:S(2)}) collective-permute-start(f32[6,8,128]{2,1,0:T(8,128)S(1)} %bitcast.20), channel_id=1, source_target_pairs={{1,2},{3,0},{2,1},{0,3},{5,6},{7,4},{6,5},{4,7},{9,10},{11,8},{10,... | collective-permute-start | bytes 73736 | tf_op jit(solution)/shard_map/ppermute | solution.py:39
  16.6 2.5 %collective-permute-start.8 = (f32[6,8,128]{2,1,0:T(8,128)S(1)}, f32[6,8,128]{2,1,0:T(8,128)S(1)}, u32[]{:S(2)}, u32[]{:S(2)}) collective-permute-start(f32[6,8,128]{2,1,0:T(8,128)S(1)} %shard_map.51.field_ref), channel_id=1, source_target_pairs={{1,2},{3,0},{2,1},{0,3},{5,6},{7,4},{6,5},{4,7},{9,10},{11,8},{10,... | collective-permute-start | bytes 73736 | tf_op jit(solution)/shard_map/ppermute | solution.py:39
  19.1 1.5 collective-permute-start.9
  32.7 2.5 %collective-permute-start.18 = (f32[6,8,128]{2,1,0:T(8,128)S(1)}, f32[6,8,128]{2,1,0:T(8,128)S(1)}, u32[]{:S(2)}, u32[]{:S(2)}) collective-permute-start(f32[6,8,128]{2,1,0:T(8,128)S(1)} %shard_map.54.field_ref), channel_id=1, source_target_pairs={{1,2},{3,0},{2,1},{0,3},{5,6},{7,4},{6,5},{4,7},{9,10},{11,8},{10,... | collective-permute-start | bytes 73736 | tf_op jit(solution)/shard_map/ppermute | solution.py:39
  35.3 1.5 collective-permute-start.19
  41.7 10.8 %all_to_all.10.sums_ref = f32[32,8,128]{2,1,0:T(8,128)S(1)} all-to-all(f32[32,8,128]{2,1,0:T(8,128)S(1)} %shard_map.56), channel_id=1, replica_groups=mesh['ta'=4,'gz'=2,'gy'=4] {'ta','gz','gy'}, dimensions={0} | all-to-all | bytes 262144 | tf_op jit(solution)/shard_map/all_to_all | solution.py:383
  54.5 1.6 collective-permute-start.26
  56.0 2.2 %collective-permute-done.23.refs_0_ = f32[6,8,128]{2,1,0:T(8,128)S(1)} collective-permute-done((f32[6,8,128]{2,1,0:T(8,128)S(1)}, f32[6,8,128]{2,1,0:T(8,128)S(1)}, u32[]{:S(2)}, u32[]{:S(2)}) %collective-permute-start.23) | collective-permute-done | bytes 24608 | tf_op jit(solution)/shard_map/ppermute | solution.py:39
  58.8 2.7 %collective-permute-start.28 = (f32[6,8,128]{2,1,0:T(8,128)S(1)}, f32[6,8,128]{2,1,0:T(8,128)S(1)}, u32[]{:S(2)}, u32[]{:S(2)}) collective-permute-start(f32[6,8,128]{2,1,0:T(8,128)S(1)} %shard_map.58.field_ref), channel_id=1, source_target_pairs={{1,2},{3,0},{2,1},{0,3},{5,6},{7,4},{6,5},{4,7},{9,10},{11,8},{10,... | collective-permute-start | bytes 73736 | tf_op jit(solution)/shard_map/ppermute | solution.py:39
  61.5 2.0 %collective-permute-start.29 = (f32[6,8,128]{2,1,0:T(8,128)S(1)}, f32[6,8,128]{2,1,0:T(8,128)S(1)}, u32[]{:S(2)}, u32[]{:S(2)}) collective-permute-start(f32[6,8,128]{2,1,0:T(8,128)S(1)} %shard_map.58.field_ref), channel_id=1, source_target_pairs={{8,16},{24,0},{16,8},{0,24},{9,17},{25,1},{17,9},{1,25},{10,18},{2... | collective-permute-start | bytes 73736 | tf_op jit(solution)/shard_map/ppermute | solution.py:39
  72.1 2.2 %collective-permute-done.33.refs_0_ = f32[6,8,128]{2,1,0:T(8,128)S(1)} collective-permute-done((f32[6,8,128]{2,1,0:T(8,128)S(1)}, f32[6,8,128]{2,1,0:T(8,128)S(1)}, u32[]{:S(2)}, u32[]{:S(2)}) %collective-permute-start.33) | collective-permute-done | bytes 24608 | tf_op jit(solution)/shard_map/ppermute | solution.py:39
  74.9 2.7 %collective-permute-start.38 = (f32[6,8,128]{2,1,0:T(8,128)S(1)}, f32[6,8,128]{2,1,0:T(8,128)S(1)}, u32[]{:S(2)}, u32[]{:S(2)}) collective-permute-start(f32[6,8,128]{2,1,0:T(8,128)S(1)} %shard_map.60.field_ref), channel_id=1, source_target_pairs={{1,2},{3,0},{2,1},{0,3},{5,6},{7,4},{6,5},{4,7},{9,10},{11,8},{10,... | collective-permute-start | bytes 73736 | tf_op jit(solution)/shard_map/ppermute | solution.py:39
  77.6 2.0 %collective-permute-start.39 = (f32[6,8,128]{2,1,0:T(8,128)S(1)}, f32[6,8,128]{2,1,0:T(8,128)S(1)}, u32[]{:S(2)}, u32[]{:S(2)}) collective-permute-start(f32[6,8,128]{2,1,0:T(8,128)S(1)} %shard_map.60.field_ref), channel_id=1, source_target_pairs={{8,16},{24,0},{16,8},{0,24},{9,17},{25,1},{17,9},{1,25},{10,18},{2... | collective-permute-start | bytes 73736 | tf_op jit(solution)/shard_map/ppermute | solution.py:39
  88.3 2.2 %collective-permute-done.43.refs_0_ = f32[6,8,128]{2,1,0:T(8,128)S(1)} collective-permute-done((f32[6,8,128]{2,1,0:T(8,128)S(1)}, f32[6,8,128]{2,1,0:T(8,128)S(1)}, u32[]{:S(2)}, u32[]{:S(2)}) %collective-permute-start.43) | collective-permute-done | bytes 24608 | tf_op jit(solution)/shard_map/ppermute | solution.py:39
  91.0 2.7 %collective-permute-start.48 = (f32[6,8,128]{2,1,0:T(8,128)S(1)}, f32[6,8,128]{2,1,0:T(8,128)S(1)}, u32[]{:S(2)}, u32[]{:S(2)}) collective-permute-start(f32[6,8,128]{2,1,0:T(8,128)S(1)} %shard_map.62.field_ref), channel_id=1, source_target_pairs={{1,2},{3,0},{2,1},{0,3},{5,6},{7,4},{6,5},{4,7},{9,10},{11,8},{10,... | collective-permute-start | bytes 73736 | tf_op jit(solution)/shard_map/ppermute | solution.py:39
  93.7 2.0 %collective-permute-start.49 = (f32[6,8,128]{2,1,0:T(8,128)S(1)}, f32[6,8,128]{2,1,0:T(8,128)S(1)}, u32[]{:S(2)}, u32[]{:S(2)}) collective-permute-start(f32[6,8,128]{2,1,0:T(8,128)S(1)} %shard_map.62.field_ref), channel_id=1, source_target_pairs={{8,16},{24,0},{16,8},{0,24},{9,17},{25,1},{17,9},{1,25},{10,18},{2... | collective-permute-start | bytes 73736 | tf_op jit(solution)/shard_map/ppermute | solution.py:39
  104.4 2.2 %collective-permute-done.53.refs_0_ = f32[6,8,128]{2,1,0:T(8,128)S(1)} collective-permute-done((f32[6,8,128]{2,1,0:T(8,128)S(1)}, f32[6,8,128]{2,1,0:T(8,128)S(1)}, u32[]{:S(2)}, u32[]{:S(2)}) %collective-permute-start.53) | collective-permute-done | bytes 24608 | tf_op jit(solution)/shard_map/ppermute | solution.py:39
  107.2 2.7 %collective-permute-start.58 = (f32[6,8,128]{2,1,0:T(8,128)S(1)}, f32[6,8,128]{2,1,0:T(8,128)S(1)}, u32[]{:S(2)}, u32[]{:S(2)}) collective-permute-start(f32[6,8,128]{2,1,0:T(8,128)S(1)} %shard_map.64.field_ref), channel_id=1, source_target_pairs={{1,2},{3,0},{2,1},{0,3},{5,6},{7,4},{6,5},{4,7},{9,10},{11,8},{10,... | collective-permute-start | bytes 73736 | tf_op jit(solution)/shard_map/ppermute | solution.py:39
  109.9 2.0 %collective-permute-start.59 = (f32[6,8,128]{2,1,0:T(8,128)S(1)}, f32[6,8,128]{2,1,0:T(8,128)S(1)}, u32[]{:S(2)}, u32[]{:S(2)}) collective-permute-start(f32[6,8,128]{2,1,0:T(8,128)S(1)} %shard_map.64.field_ref), channel_id=1, source_target_pairs={{8,16},{24,0},{16,8},{0,24},{9,17},{25,1},{17,9},{1,25},{10,18},{2... | collective-permute-start | bytes 73736 | tf_op jit(solution)/shard_map/ppermute | solution.py:39
  120.6 2.2 %collective-permute-done.63.refs_0_ = f32[6,8,128]{2,1,0:T(8,128)S(1)} collective-permute-done((f32[6,8,128]{2,1,0:T(8,128)S(1)}, f32[6,8,128]{2,1,0:T(8,128)S(1)}, u32[]{:S(2)}, u32[]{:S(2)}) %collective-permute-start.63) | collective-permute-done | bytes 24608 | tf_op jit(solution)/shard_map/ppermute | solution.py:39
  123.3 2.7 %collective-permute-start.68 = (f32[6,8,128]{2,1,0:T(8,128)S(1)}, f32[6,8,128]{2,1,0:T(8,128)S(1)}, u32[]{:S(2)}, u32[]{:S(2)}) collective-permute-start(f32[6,8,128]{2,1,0:T(8,128)S(1)} %shard_map.66.field_ref), channel_id=1, source_target_pairs={{1,2},{3,0},{2,1},{0,3},{5,6},{7,4},{6,5},{4,7},{9,10},{11,8},{10,... | collective-permute-start | bytes 73736 | tf_op jit(solution)/shard_map/ppermute | solution.py:39
  126.0 2.0 %collective-permute-start.69 = (f32[6,8,128]{2,1,0:T(8,128)S(1)}, f32[6,8,128]{2,1,0:T(8,128)S(1)}, u32[]{:S(2)}, u32[]{:S(2)}) collective-permute-start(f32[6,8,128]{2,1,0:T(8,128)S(1)} %shard_map.66.field_ref), channel_id=1, source_target_pairs={{8,16},{24,0},{16,8},{0,24},{9,17},{25,1},{17,9},{1,25},{10,18},{2... | collective-permute-start | bytes 73736 | tf_op jit(solution)/shard_map/ppermute | solution.py:39
  136.7 2.2 %collective-permute-done.73.refs_0_ = f32[6,8,128]{2,1,0:T(8,128)S(1)} collective-permute-done((f32[6,8,128]{2,1,0:T(8,128)S(1)}, f32[6,8,128]{2,1,0:T(8,128)S(1)}, u32[]{:S(2)}, u32[]{:S(2)}) %collective-permute-start.73) | collective-permute-done | bytes 24608 | tf_op jit(solution)/shard_map/ppermute | solution.py:39
  139.4 2.7 %collective-permute-start.78 = (f32[6,8,128]{2,1,0:T(8,128)S(1)}, f32[6,8,128]{2,1,0:T(8,128)S(1)}, u32[]{:S(2)}, u32[]{:S(2)}) collective-permute-start(f32[6,8,128]{2,1,0:T(8,128)S(1)} %shard_map.68.field_ref), channel_id=1, source_target_pairs={{1,2},{3,0},{2,1},{0,3},{5,6},{7,4},{6,5},{4,7},{9,10},{11,8},{10,... | collective-permute-start | bytes 73736 | tf_op jit(solution)/shard_map/ppermute | solution.py:39
  142.1 2.0 %collective-permute-start.79 = (f32[6,8,128]{2,1,0:T(8,128)S(1)}, f32[6,8,128]{2,1,0:T(8,128)S(1)}, u32[]{:S(2)}, u32[]{:S(2)}) collective-permute-start(f32[6,8,128]{2,1,0:T(8,128)S(1)} %shard_map.68.field_ref), channel_id=1, source_target_pairs={{8,16},{24,0},{16,8},{0,24},{9,17},{25,1},{17,9},{1,25},{10,18},{2... | collective-permute-start | bytes 73736 | tf_op jit(solution)/shard_map/ppermute | solution.py:39
  149.5 10.1 %all_to_all.11.sums_ref = f32[32,8,128]{2,1,0:T(8,128)S(1)} all-to-all(f32[32,8,128]{2,1,0:T(8,128)S(1)} %shard_map.70), channel_id=1, replica_groups=mesh['ta'=4,'gz'=2,'gy'=4] {'ta','gz','gy'}, dimensions={0} | all-to-all | bytes 262144 | tf_op jit(solution)/shard_map/all_to_all | solution.py:383
  162.4 1.6 collective-permute-start.86
  164.0 2.6 %collective-permute-done.83.refs_0_ = f32[6,8,128]{2,1,0:T(8,128)S(1)} collective-permute-done((f32[6,8,128]{2,1,0:T(8,128)}, f32[6,8,128]{2,1,0:T(8,128)S(1)}, u32[]{:S(2)}, u32[]{:S(2)}) %collective-permute-start.83) | collective-permute-done | bytes 24608 | tf_op jit(solution)/shard_map/ppermute | solution.py:39
  167.7 2.8 %collective-permute-start.88 = (f32[6,8,128]{2,1,0:T(8,128)S(1)}, f32[6,8,128]{2,1,0:T(8,128)S(1)}, u32[]{:S(2)}, u32[]{:S(2)}) collective-permute-start(f32[6,8,128]{2,1,0:T(8,128)S(1)} %shard_map.72.field_ref), channel_id=1, source_target_pairs={{1,2},{3,0},{2,1},{0,3},{5,6},{7,4},{6,5},{4,7},{9,10},{11,8},{10,... | collective-permute-start | bytes 73736 | tf_op jit(solution)/shard_map/ppermute | solution.py:39
  170.5 2.0 %collective-permute-start.89 = (f32[6,8,128]{2,1,0:T(8,128)S(1)}, f32[6,8,128]{2,1,0:T(8,128)S(1)}, u32[]{:S(2)}, u32[]{:S(2)}) collective-permute-start(f32[6,8,128]{2,1,0:T(8,128)S(1)} %shard_map.72.field_ref), channel_id=1, source_target_pairs={{8,16},{24,0},{16,8},{0,24},{9,17},{25,1},{17,9},{1,25},{10,18},{2... | collective-permute-start | bytes 73736 | tf_op jit(solution)/shard_map/ppermute | solution.py:39
  (194 shorter events, 89.3 us)
Async XLA Ops:
  2.8 8.3 %collective-permute-start = (bf16[2,2,18,8,128]{4,3,2,1,0:T(8,128)(2,1)S(1)}, bf16[2,2,18,8,128]{4,3,2,1,0:T(8,128)(2,1)S(1)}, u32[]{:S(2)}, u32[]{:S(2)}) collective-permute-start(bf16[2,2,18,8,128]{4,3,2,1,0:T(8,128)(2,1)S(1)} %pad_maximum_fusion), channel_id=1, source_target_pairs={{0,8},{8,16},{16,24},{24,0},{1,9},{9,17},{17,25},{25,1},{2,10},{10... | collective-permute-start | bytes 442376 | tf_op jit(solution)/shard_map/ppermute | solution.py:32
  5.9 6.6 %collective-permute-start.1 = (bf16[2,2,18,8,128]{4,3,2,1,0:T(8,128)(2,1)S(1)}, bf16[2,2,18,8,128]{4,3,2,1,0:T(8,128)(2,1)S(1)}, u32[]{:S(2)}, u32[]{:S(2)}) collective-permute-start(bf16[2,2,18,8,128]{4,3,2,1,0:T(8,128)(2,1)S(1)} %pad_maximum_fusion.1), channel_id=1, source_target_pairs={{0,4},{4,0},{1,5},{5,1},{2,6},{6,2},{3,7},{7,3},{8,12},{12,8},{9,1... | collective-permute-start | bytes 442376 | tf_op jit(solution)/shard_map/ppermute | solution.py:32
  6.0 8.6 %collective-permute-start.2 = (bf16[2,2,18,8,128]{4,3,2,1,0:T(8,128)(2,1)S(1)}, bf16[2,2,18,8,128]{4,3,2,1,0:T(8,128)(2,1)S(1)}, u32[]{:S(2)}, u32[]{:S(2)}) collective-permute-start(bf16[2,2,18,8,128]{4,3,2,1,0:T(8,128)(2,1)S(1)} %pad_maximum_fusion.2), channel_id=1, source_target_pairs={{0,1},{1,2},{2,3},{3,0},{4,5},{5,6},{6,7},{7,4},{8,9},{9,10},{10,1... | collective-permute-start | bytes 442376 | tf_op jit(solution)/shard_map/ppermute | solution.py:32
  7.6 7.9 %collective-permute-start.3 = (f32[6,8,128]{2,1,0:T(8,128)S(1)}, f32[6,8,128]{2,1,0:T(8,128)S(1)}, u32[]{:S(2)}, u32[]{:S(2)}) collective-permute-start(f32[6,8,128]{2,1,0:T(8,128)S(1)} %bitcast.20), channel_id=1, source_target_pairs={{1,2},{3,0},{2,1},{0,3},{5,6},{7,4},{6,5},{4,7},{9,10},{11,8},{10,... | collective-permute-start | bytes 73736 | tf_op jit(solution)/shard_map/ppermute | solution.py:39
  9.9 5.7 %collective-permute-start.4 = (f32[6,8,128]{2,1,0:T(8,128)S(1)}, f32[6,8,128]{2,1,0:T(8,128)S(1)}, u32[]{:S(2)}, u32[]{:S(2)}) collective-permute-start(f32[6,8,128]{2,1,0:T(8,128)S(1)} %bitcast.21), channel_id=1, source_target_pairs={{8,16},{24,0},{16,8},{0,24},{9,17},{25,1},{17,9},{1,25},{10,18},{2... | collective-permute-start | bytes 73736 | tf_op jit(solution)/shard_map/ppermute | solution.py:39
  16.6 7.0 %collective-permute-start.8 = (f32[6,8,128]{2,1,0:T(8,128)S(1)}, f32[6,8,128]{2,1,0:T(8,128)S(1)}, u32[]{:S(2)}, u32[]{:S(2)}) collective-permute-start(f32[6,8,128]{2,1,0:T(8,128)S(1)} %shard_map.51.field_ref), channel_id=1, source_target_pairs={{1,2},{3,0},{2,1},{0,3},{5,6},{7,4},{6,5},{4,7},{9,10},{11,8},{10,... | collective-permute-start | bytes 73736 | tf_op jit(solution)/shard_map/ppermute | solution.py:39
  19.1 4.7 %collective-permute-start.9 = (f32[6,8,128]{2,1,0:T(8,128)S(1)}, f32[6,8,128]{2,1,0:T(8,128)S(1)}, u32[]{:S(2)}, u32[]{:S(2)}) collective-permute-start(f32[6,8,128]{2,1,0:T(8,128)S(1)} %shard_map.51.field_ref), channel_id=1, source_target_pairs={{8,16},{24,0},{16,8},{0,24},{9,17},{25,1},{17,9},{1,25},{10,18},{2... | collective-permute-start | bytes 73736 | tf_op jit(solution)/shard_map/ppermute | solution.py:39
  25.4 5.7 %collective-permute-start.13 = (f32[6,8,128]{2,1,0:T(8,128)S(1)}, f32[6,8,128]{2,1,0:T(8,128)S(1)}, u32[]{:S(2)}, u32[]{:S(2)}) collective-permute-start(f32[6,8,128]{2,1,0:T(8,128)S(1)} %shard_map.53.field_ref.start_ref.refs_1_.v1), channel_id=1, source_target_pairs={{1,2},{3,0},{2,1},{0,3},{5,6},{7,4},{6,5},{4,7},{9,10},{11,8},{10,... | collective-permute-start | bytes 73736 | tf_op jit(solution)/shard_map/ppermute | solution.py:39
  26.5 4.7 %collective-permute-start.14 = (f32[6,8,128]{2,1,0:T(8,128)S(1)}, f32[6,8,128]{2,1,0:T(8,128)S(1)}, u32[]{:S(2)}, u32[]{:S(2)}) collective-permute-start(f32[6,8,128]{2,1,0:T(8,128)S(1)} %shard_map.53.field_ref.start_ref.refs_1_.v1), channel_id=1, source_target_pairs={{8,16},{24,0},{16,8},{0,24},{9,17},{25,1},{17,9},{1,25},{10,18},{2... | collective-permute-start | bytes 73736 | tf_op jit(solution)/shard_map/ppermute | solution.py:39
  32.7 6.2 %collective-permute-start.18 = (f32[6,8,128]{2,1,0:T(8,128)S(1)}, f32[6,8,128]{2,1,0:T(8,128)S(1)}, u32[]{:S(2)}, u32[]{:S(2)}) collective-permute-start(f32[6,8,128]{2,1,0:T(8,128)S(1)} %shard_map.54.field_ref), channel_id=1, source_target_pairs={{1,2},{3,0},{2,1},{0,3},{5,6},{7,4},{6,5},{4,7},{9,10},{11,8},{10,... | collective-permute-start | bytes 73736 | tf_op jit(solution)/shard_map/ppermute | solution.py:39
  35.3 4.7 %collective-permute-start.19 = (f32[6,8,128]{2,1,0:T(8,128)S(1)}, f32[6,8,128]{2,1,0:T(8,128)S(1)}, u32[]{:S(2)}, u32[]{:S(2)}) collective-permute-start(f32[6,8,128]{2,1,0:T(8,128)S(1)} %shard_map.54.field_ref), channel_id=1, source_target_pairs={{8,16},{24,0},{16,8},{0,24},{9,17},{25,1},{17,9},{1,25},{10,18},{2... | collective-permute-start | bytes 73736 | tf_op jit(solution)/shard_map/ppermute | solution.py:39
  52.5 5.7 %collective-permute-start.23 = (f32[6,8,128]{2,1,0:T(8,128)S(1)}, f32[6,8,128]{2,1,0:T(8,128)S(1)}, u32[]{:S(2)}, u32[]{:S(2)}) collective-permute-start(f32[6,8,128]{2,1,0:T(8,128)S(1)} %get-tuple-element.4.field_ref.start_ref.refs_6_.refs_2_), channel_id=1, source_target_pairs={{1,2},{3,0},{2,1},{0,3},{5,6},{7,4},{6,5},{4,7},{9,10},{11,8},{10,... | collective-permute-start | bytes 73736 | tf_op jit(solution)/shard_map/ppermute | solution.py:39
  58.8 6.6 %collective-permute-start.28 = (f32[6,8,128]{2,1,0:T(8,128)S(1)}, f32[6,8,128]{2,1,0:T(8,128)S(1)}, u32[]{:S(2)}, u32[]{:S(2)}) collective-permute-start(f32[6,8,128]{2,1,0:T(8,128)S(1)} %shard_map.58.field_ref), channel_id=1, source_target_pairs={{1,2},{3,0},{2,1},{0,3},{5,6},{7,4},{6,5},{4,7},{9,10},{11,8},{10,... | collective-permute-start | bytes 73736 | tf_op jit(solution)/shard_map/ppermute | solution.py:39
  61.5 4.7 %collective-permute-start.29 = (f32[6,8,128]{2,1,0:T(8,128)S(1)}, f32[6,8,128]{2,1,0:T(8,128)S(1)}, u32[]{:S(2)}, u32[]{:S(2)}) collective-permute-start(f32[6,8,128]{2,1,0:T(8,128)S(1)} %shard_map.58.field_ref), channel_id=1, source_target_pairs={{8,16},{24,0},{16,8},{0,24},{9,17},{25,1},{17,9},{1,25},{10,18},{2... | collective-permute-start | bytes 73736 | tf_op jit(solution)/shard_map/ppermute | solution.py:39
  68.7 5.7 %collective-permute-start.33 = (f32[6,8,128]{2,1,0:T(8,128)S(1)}, f32[6,8,128]{2,1,0:T(8,128)S(1)}, u32[]{:S(2)}, u32[]{:S(2)}) collective-permute-start(f32[6,8,128]{2,1,0:T(8,128)S(1)} %shard_map.59.field_ref.start_ref.refs_6_.refs_3_), channel_id=1, source_target_pairs={{1,2},{3,0},{2,1},{0,3},{5,6},{7,4},{6,5},{4,7},{9,10},{11,8},{10,... | collective-permute-start | bytes 73736 | tf_op jit(solution)/shard_map/ppermute | solution.py:39
  74.9 6.6 %collective-permute-start.38 = (f32[6,8,128]{2,1,0:T(8,128)S(1)}, f32[6,8,128]{2,1,0:T(8,128)S(1)}, u32[]{:S(2)}, u32[]{:S(2)}) collective-permute-start(f32[6,8,128]{2,1,0:T(8,128)S(1)} %shard_map.60.field_ref), channel_id=1, source_target_pairs={{1,2},{3,0},{2,1},{0,3},{5,6},{7,4},{6,5},{4,7},{9,10},{11,8},{10,... | collective-permute-start | bytes 73736 | tf_op jit(solution)/shard_map/ppermute | solution.py:39
  84.8 5.7 %collective-permute-start.43 = (f32[6,8,128]{2,1,0:T(8,128)S(1)}, f32[6,8,128]{2,1,0:T(8,128)S(1)}, u32[]{:S(2)}, u32[]{:S(2)}) collective-permute-start(f32[6,8,128]{2,1,0:T(8,128)S(1)} %shard_map.61.field_ref.start_ref.refs_6_.refs_4_), channel_id=1, source_target_pairs={{1,2},{3,0},{2,1},{0,3},{5,6},{7,4},{6,5},{4,7},{9,10},{11,8},{10,... | collective-permute-start | bytes 73736 | tf_op jit(solution)/shard_map/ppermute | solution.py:39
  86.1 4.7 %collective-permute-start.44 = (f32[6,8,128]{2,1,0:T(8,128)S(1)}, f32[6,8,128]{2,1,0:T(8,128)S(1)}, u32[]{:S(2)}, u32[]{:S(2)}) collective-permute-start(f32[6,8,128]{2,1,0:T(8,128)S(1)} %shard_map.61.field_ref.start_ref.refs_6_.refs_4_), channel_id=1, source_target_pairs={{8,16},{24,0},{16,8},{0,24},{9,17},{25,1},{17,9},{1,25},{10,18},{2... | collective-permute-start | bytes 73736 | tf_op jit(solution)/shard_map/ppermute | solution.py:39
  91.0 6.6 %collective-permute-start.48 = (f32[6,8,128]{2,1,0:T(8,128)S(1)}, f32[6,8,128]{2,1,0:T(8,128)S(1)}, u32[]{:S(2)}, u32[]{:S(2)}) collective-permute-start(f32[6,8,128]{2,1,0:T(8,128)S(1)} %shard_map.62.field_ref), channel_id=1, source_target_pairs={{1,2},{3,0},{2,1},{0,3},{5,6},{7,4},{6,5},{4,7},{9,10},{11,8},{10,... | collective-permute-start | bytes 73736 | tf_op jit(solution)/shard_map/ppermute | solution.py:39
  93.7 4.7 %collective-permute-start.49 = (f32[6,8,128]{2,1,0:T(8,128)S(1)}, f32[6,8,128]{2,1,0:T(8,128)S(1)}, u32[]{:S(2)}, u32[]{:S(2)}) collective-permute-start(f32[6,8,128]{2,1,0:T(8,128)S(1)} %shard_map.62.field_ref), channel_id=1, source_target_pairs={{8,16},{24,0},{16,8},{0,24},{9,17},{25,1},{17,9},{1,25},{10,18},{2... | collective-permute-start | bytes 73736 | tf_op jit(solution)/shard_map/ppermute | solution.py:39
  100.9 5.7 %collective-permute-start.53 = (f32[6,8,128]{2,1,0:T(8,128)S(1)}, f32[6,8,128]{2,1,0:T(8,128)S(1)}, u32[]{:S(2)}, u32[]{:S(2)}) collective-permute-start(f32[6,8,128]{2,1,0:T(8,128)S(1)} %shard_map.63.field_ref.start_ref.refs_6_.refs_5_), channel_id=1, source_target_pairs={{1,2},{3,0},{2,1},{0,3},{5,6},{7,4},{6,5},{4,7},{9,10},{11,8},{10,... | collective-permute-start | bytes 73736 | tf_op jit(solution)/shard_map/ppermute | solution.py:39
  102.2 4.7 %collective-permute-start.54 = (f32[6,8,128]{2,1,0:T(8,128)S(1)}, f32[6,8,128]{2,1,0:T(8,128)S(1)}, u32[]{:S(2)}, u32[]{:S(2)}) collective-permute-start(f32[6,8,128]{2,1,0:T(8,128)S(1)} %shard_map.63.field_ref.start_ref.refs_6_.refs_5_), channel_id=1, source_target_pairs={{8,16},{24,0},{16,8},{0,24},{9,17},{25,1},{17,9},{1,25},{10,18},{2... | collective-permute-start | bytes 73736 | tf_op jit(solution)/shard_map/ppermute | solution.py:39
  107.2 6.6 %collective-permute-start.58 = (f32[6,8,128]{2,1,0:T(8,128)S(1)}, f32[6,8,128]{2,1,0:T(8,128)S(1)}, u32[]{:S(2)}, u32[]{:S(2)}) collective-permute-start(f32[6,8,128]{2,1,0:T(8,128)S(1)} %shard_map.64.field_ref), channel_id=1, source_target_pairs={{1,2},{3,0},{2,1},{0,3},{5,6},{7,4},{6,5},{4,7},{9,10},{11,8},{10,... | collective-permute-start | bytes 73736 | tf_op jit(solution)/shard_map/ppermute | solution.py:39
  109.9 4.7 %collective-permute-start.59 = (f32[6,8,128]{2,1,0:T(8,128)S(1)}, f32[6,8,128]{2,1,0:T(8,128)S(1)}, u32[]{:S(2)}, u32[]{:S(2)}) collective-permute-start(f32[6,8,128]{2,1,0:T(8,128)S(1)} %shard_map.64.field_ref), channel_id=1, source_target_pairs={{8,16},{24,0},{16,8},{0,24},{9,17},{25,1},{17,9},{1,25},{10,18},{2... | collective-permute-start | bytes 73736 | tf_op jit(solution)/shard_map/ppermute | solution.py:39
  117.1 5.7 %collective-permute-start.63 = (f32[6,8,128]{2,1,0:T(8,128)S(1)}, f32[6,8,128]{2,1,0:T(8,128)S(1)}, u32[]{:S(2)}, u32[]{:S(2)}) collective-permute-start(f32[6,8,128]{2,1,0:T(8,128)S(1)} %shard_map.65.field_ref.start_ref.refs_6_), channel_id=1, source_target_pairs={{1,2},{3,0},{2,1},{0,3},{5,6},{7,4},{6,5},{4,7},{9,10},{11,8},{10,... | collective-permute-start | bytes 73736 | tf_op jit(solution)/shard_map/ppermute | solution.py:39
  123.3 6.6 %collective-permute-start.68 = (f32[6,8,128]{2,1,0:T(8,128)S(1)}, f32[6,8,128]{2,1,0:T(8,128)S(1)}, u32[]{:S(2)}, u32[]{:S(2)}) collective-permute-start(f32[6,8,128]{2,1,0:T(8,128)S(1)} %shard_map.66.field_ref), channel_id=1, source_target_pairs={{1,2},{3,0},{2,1},{0,3},{5,6},{7,4},{6,5},{4,7},{9,10},{11,8},{10,... | collective-permute-start | bytes 73736 | tf_op jit(solution)/shard_map/ppermute | solution.py:39
  133.2 5.7 %collective-permute-start.73 = (f32[6,8,128]{2,1,0:T(8,128)S(1)}, f32[6,8,128]{2,1,0:T(8,128)S(1)}, u32[]{:S(2)}, u32[]{:S(2)}) collective-permute-start(f32[6,8,128]{2,1,0:T(8,128)S(1)} %shard_map.67.field_ref.start_ref.refs_7_), channel_id=1, source_target_pairs={{1,2},{3,0},{2,1},{0,3},{5,6},{7,4},{6,5},{4,7},{9,10},{11,8},{10,... | collective-permute-start | bytes 73736 | tf_op jit(solution)/shard_map/ppermute | solution.py:39
  139.4 6.6 %collective-permute-start.78 = (f32[6,8,128]{2,1,0:T(8,128)S(1)}, f32[6,8,128]{2,1,0:T(8,128)S(1)}, u32[]{:S(2)}, u32[]{:S(2)}) collective-permute-start(f32[6,8,128]{2,1,0:T(8,128)S(1)} %shard_map.68.field_ref), channel_id=1, source_target_pairs={{1,2},{3,0},{2,1},{0,3},{5,6},{7,4},{6,5},{4,7},{9,10},{11,8},{10,... | collective-permute-start | bytes 73736 | tf_op jit(solution)/shard_map/ppermute | solution.py:39
  160.7 5.9 %collective-permute-start.83 = (f32[6,8,128]{2,1,0:T(8,128)}, f32[6,8,128]{2,1,0:T(8,128)S(1)}, u32[]{:S(2)}, u32[]{:S(2)}) collective-permute-start(f32[6,8,128]{2,1,0:T(8,128)} %shard_map.71.field_ref.start_ref), channel_id=1, source_target_pairs={{1,2},{3,0},{2,1},{0,3},{5,6},{7,4},{6,5},{4,7},{9,10},{11,8},{10,... | collective-permute-start | bytes 73736 | tf_op jit(solution)/shard_map/ppermute | solution.py:39
  161.8 4.9 %collective-permute-start.84 = (f32[6,8,128]{2,1,0:T(8,128)}, f32[6,8,128]{2,1,0:T(8,128)S(1)}, u32[]{:S(2)}, u32[]{:S(2)}) collective-permute-start(f32[6,8,128]{2,1,0:T(8,128)} %shard_map.71.field_ref.start_ref), channel_id=1, source_target_pairs={{8,16},{24,0},{16,8},{0,24},{9,17},{25,1},{17,9},{1,25},{10,18},{2... | collective-permute-start | bytes 73736 | tf_op jit(solution)/shard_map/ppermute | solution.py:39
  167.7 6.7 %collective-permute-start.88 = (f32[6,8,128]{2,1,0:T(8,128)S(1)}, f32[6,8,128]{2,1,0:T(8,128)S(1)}, u32[]{:S(2)}, u32[]{:S(2)}) collective-permute-start(f32[6,8,128]{2,1,0:T(8,128)S(1)} %shard_map.72.field_ref), channel_id=1, source_target_pairs={{1,2},{3,0},{2,1},{0,3},{5,6},{7,4},{6,5},{4,7},{9,10},{11,8},{10,... | collective-permute-start | bytes 73736 | tf_op jit(solution)/shard_map/ppermute | solution.py:39
  170.5 4.7 %collective-permute-start.89 = (f32[6,8,128]{2,1,0:T(8,128)S(1)}, f32[6,8,128]{2,1,0:T(8,128)S(1)}, u32[]{:S(2)}, u32[]{:S(2)}) collective-permute-start(f32[6,8,128]{2,1,0:T(8,128)S(1)} %shard_map.72.field_ref), channel_id=1, source_target_pairs={{8,16},{24,0},{16,8},{0,24},{9,17},{25,1},{17,9},{1,25},{10,18},{2... | collective-permute-start | bytes 73736 | tf_op jit(solution)/shard_map/ppermute | solution.py:39
  (63 other events, 229.0 us)
